TPU v7x, 32 devices: a whole 2x2x4 slice. The times are simulated.
32 devices in a mesh: ens: 2 (over y), gx: 4 (over z), col: 2 (over x), gz: 2 (over core).
Axes of the slice: x: 2, y: 2, z: 4, core: 2. Of those that a mesh axis runs over, the one named last changes fastest.
Arguments:
- checkpoints: bfloat16 [8, 3, 32, 8, 256], P(('ens', 'col'), None, 'gz', 'gx'), parts along dimension 0, may hold values from -3 to 3
- obs_values: float32 [8, 32, 8, 256], P('ens', 'gz', 'gx', 'col'), parts along dimension 0, may hold values from -3 to 3
- obs_mask: int32 [8, 32, 8, 256], P('ens', 'gz', 'gx', 'col'), parts along dimension 0, may hold values 0 or 1
- drag: float32 [64], P(('ens', 'gz')), parts along dimension 0, may hold values from 0.05 to 0.5
Outputs:
- grad_init: float32 [6, 32, 8, 256], P('ens', 'gz', 'gx', 'col'), parts along dimension 0
- cost_levels: float32 [64], P(('ens', 'gz')), parts along dimension 0
- drag_grad: float32 [64], P(('ens', 'gz')), parts along dimension 0
There are 2 independent parts, one for each index of `ens`. A program takes and returns all parts, laid end to end along the dimension named above; each array names one. Nothing has to cross between parts.
All inputs are finite; a program needn't handle non-finite values. No bound on the sum of `obs_mask` on one device may be relied on, other than what follows from the above.
Results may differ from a plain program's by a relative error of at most 0.0003.
Values may be sent and summed in bfloat16 or wider, within the bound.
A program may use at most 64 MiB of HBM per device.

v0:
```python
import jax
import jax.numpy as jnp
from jax import lax
from jax.sharding import PartitionSpec as P

SEG = 2


time_step = 0.1
viscosity = 0.05
vertical_mix = 0.2


def with_halo(x, sides, width):
    for axis, dim in sides:
        devices, length = (lax.axis_size(axis), x.shape[dim])
        up = [(i, (i + 1) % devices) for i in range(devices - 1)]
        down = [(j, i) for i, j in up]
        last = lax.slice_in_dim(x, length - width, length, axis=dim)
        initial = lax.slice_in_dim(x, 0, width, axis=dim)
        before = lax.ppermute(last, axis, up)
        after = lax.ppermute(initial, axis, down)
        x = jnp.concatenate([before, x, after], axis=dim)
    return x


def passed_along(block, axis, distance):
    devices = range(lax.axis_size(axis))
    route = [(i - distance, i) for i in devices if i - distance in devices]
    return lax.ppermute(block, axis, route)


def along_cols(a):
    return 0.5 * (a[:, 1:-1, 2:] - a[:, 1:-1, :-2])


def along_rows(a):
    return 0.5 * (a[:, 2:, 1:-1] - a[:, :-2, 1:-1])


def laplace(a):
    return (
        a[:, 2:, 1:-1] + a[:, :-2, 1:-1] + a[:, 1:-1, 2:] + a[:, 1:-1, :-2] - 4.0 * a[:, 1:-1, 1:-1]
    )


def advance(padded, drag, coriolis):
    levels = padded[:, 1:-1]
    thick, zonal, merid = (levels[0], levels[1], levels[2])
    centre = padded[:, 1:-1, 1:-1, 1:-1]
    h_c, u_c, v_c = (centre[0], centre[1], centre[2])
    rot = coriolis[None, :, None]
    rate = drag[:, None, None]
    vert = padded[:, 2:, 1:-1, 1:-1] + padded[:, :-2, 1:-1, 1:-1] - 2.0 * centre
    u_new = (
        u_c
        + time_step
        * (
            -along_cols(thick)
            - u_c * along_cols(zonal)
            - v_c * along_rows(zonal)
            + rot * v_c
            - rate * u_c
        )
        + viscosity * laplace(zonal)
    )
    v_new = (
        v_c
        + time_step
        * (
            -along_rows(thick)
            - u_c * along_cols(merid)
            - v_c * along_rows(merid)
            - rot * u_c
            - rate * v_c
        )
        + viscosity * laplace(merid)
    )
    h_new = (
        h_c
        - time_step
        * (
            along_cols(zonal)
            + along_rows(merid)
            + along_cols(thick * zonal)
            + along_rows(thick * merid)
        )
        + viscosity * laplace(thick)
    )
    return jnp.stack([h_new, u_new, v_new]) + vertical_mix * vert


def extend(state):
    return with_halo(state, (("gx", 2), ("col", 3), ("gz", 1)), 1)


def halo_back(cot):
    inner = cot[:, 1:-1, 1:-1, 1:-1]
    below = passed_along(cot[:, 0, 1:-1, 1:-1], "gz", -1)
    above = passed_along(cot[:, -1, 1:-1, 1:-1], "gz", 1)
    inner = inner.at[:, -1].add(below).at[:, 0].add(above)
    south = passed_along(cot[:, 1:-1, 0, 1:-1], "gx", -1)
    north = passed_along(cot[:, 1:-1, -1, 1:-1], "gx", 1)
    inner = inner.at[:, :, -1].add(south).at[:, :, 0].add(north)
    west = passed_along(cot[:, 1:-1, 1:-1, 0], "col", -1)
    east = passed_along(cot[:, 1:-1, 1:-1, -1], "col", 1)
    return inner.at[:, :, :, -1].add(west).at[:, :, :, 0].add(east)


def on_device(checkpoints, obs_values, obs_mask, drag):
    lat_count = obs_values.shape[2]
    lon_count = obs_values.shape[3]
    segments = obs_values.shape[0]
    total_lat = lat_count * lax.axis_size("gx")
    total_lon = lon_count * lax.axis_size("col")
    rows = (lax.axis_index("gx") * lat_count + jnp.arange(lat_count)).astype(jnp.float32)
    cols = (lax.axis_index("col") * lon_count + jnp.arange(lon_count)).astype(jnp.float32)
    coriolis = 0.2 + 0.1 * rows / total_lat
    weight = (1.0 + 2.0 * rows / total_lat)[:, None] * (1.0 + 2.0 * cols / total_lon)[None, :]
    owned_cols = lax.all_to_all(checkpoints, "col", split_axis=4, concat_axis=0, tiled=True)

    def local(padded, rate):
        return advance(padded, rate, coriolis)

    levels = drag.shape[0]
    adjoint = jnp.zeros((3, levels, lat_count, lon_count), jnp.float32)
    cost = jnp.zeros((levels,), jnp.float32)
    drag_total = jnp.zeros((levels,), jnp.float32)
    for seg in reversed(range(segments)):
        state = owned_cols[seg].astype(jnp.float32)
        pads = []
        for step in range(SEG):
            padded = extend(state)
            pads.append(padded)
            state = advance(padded, drag, coriolis)
        resid = state[0] - obs_values[seg]
        forcing = weight[None] * obs_mask[seg].astype(jnp.float32) * resid
        seg_cost = 0.5 * jnp.sum(forcing * resid, axis=(1, 2))
        adjoint = adjoint.at[0].add(forcing)
        seg_drag = jnp.zeros((levels,), jnp.float32)
        for step in reversed(range(SEG)):
            unused, pull = jax.vjp(local, pads[step], drag)
            cot_pad, cot_drag = pull(adjoint)
            seg_drag = seg_drag + cot_drag
            adjoint = halo_back(cot_pad)
        summed_drag, summed_cost = lax.psum((seg_drag, seg_cost), ("gx", "col"))
        drag_total = drag_total + summed_drag
        cost = cost + summed_cost
    scale = 1.0 / (total_lat * total_lon)
    return (adjoint, cost * scale, drag_total * scale)


def solution(mesh):
    return jax.shard_map(
        on_device,
        mesh=mesh,
        in_specs=(
            P(("ens", "col"), None, "gz", "gx", None),
            P("ens", "gz", "gx", "col"),
            P("ens", "gz", "gx", "col"),
            P(("ens", "gz")),
        ),
        out_specs=(P("ens", "gz", "gx", "col"), P(("ens", "gz")), P(("ens", "gz"))),
        check_vma=False,
    )
```

profile of v0, /device:TPU:1, one launch (start us, length us, event | category | flops | bytes accessed | tf_op | source)
XLA Modules:
  0.0 333.4 jit_solution(2285676061232083874)
XLA Ops:
  0.6 2.4 copy.1074
  3.0 1.5 reshape.2001
  4.5 3.5 %all-to-all-start = ((bf16[2,2,12288]{2,1,0:T(2,128)(2,1)}), bf16[2,2,12288]{2,1,0:T(2,128)(2,1)S(1)}, u32[]{:S(2)}, u32[]{:S(2)}) async-start(bf16[2,2,12288]{2,1,0:T(2,128)(2,1)} %reshape.2001), calls=%async_computation | async-start | bytes 196608 | tf_op jit(solution)/shard_map/all_to_all | solution.py:120
  9.7 1.9 all-to-all-done
  13.2 3.5 %collective-permute-start = (f32[3,16,1,128]{3,1,2,0:T(8,128)S(1)}, f32[3,16,1,128]{3,1,2,0:T(8,128)S(1)}, u32[]{:S(2)}, u32[]{:S(2)}) collective-permute-start(f32[3,16,1,128]{3,1,2,0:T(8,128)S(1)} %get-tuple-element.1053), channel_id=1, source_target_pairs={{0,4},{4,8},{8,12},{1,5},{5,9},{9,13},{2,6},{6,10},{10,14},{3,7},{... | collective-permute-start | bytes 73736 | tf_op jit(solution)/shard_map/ppermute | solution.py:21
  17.9 4.0 %collective-permute-start.24 = (f32[3,16,1,128]{3,1,2,0:T(8,128)S(1)}, f32[3,16,1,128]{3,1,2,0:T(8,128)S(1)}, u32[]{:S(2)}, u32[]{:S(2)}) collective-permute-start(f32[3,16,1,128]{3,1,2,0:T(8,128)S(1)} %get-tuple-element.1057), channel_id=1, source_target_pairs={{0,4},{4,8},{8,12},{1,5},{5,9},{9,13},{2,6},{6,10},{10,14},{3,7},{... | collective-permute-start | bytes 73736 | tf_op jit(solution)/shard_map/ppermute | solution.py:21
  23.2 4.0 %collective-permute-start.48 = (f32[3,16,1,128]{3,1,2,0:T(8,128)S(1)}, f32[3,16,1,128]{3,1,2,0:T(8,128)S(1)}, u32[]{:S(2)}, u32[]{:S(2)}) collective-permute-start(f32[3,16,1,128]{3,1,2,0:T(8,128)S(1)} %get-tuple-element.1061), channel_id=1, source_target_pairs={{0,4},{4,8},{8,12},{1,5},{5,9},{9,13},{2,6},{6,10},{10,14},{3,7},{... | collective-permute-start | bytes 73736 | tf_op jit(solution)/shard_map/ppermute | solution.py:21
  28.6 4.0 %collective-permute-start.72 = (f32[3,16,1,128]{3,1,2,0:T(8,128)S(1)}, f32[3,16,1,128]{3,1,2,0:T(8,128)S(1)}, u32[]{:S(2)}, u32[]{:S(2)}) collective-permute-start(f32[3,16,1,128]{3,1,2,0:T(8,128)S(1)} %get-tuple-element.1065), channel_id=1, source_target_pairs={{0,4},{4,8},{8,12},{1,5},{5,9},{9,13},{2,6},{6,10},{10,14},{3,7},{... | collective-permute-start | bytes 73736 | tf_op jit(solution)/shard_map/ppermute | solution.py:21
  34.0 2.0 collective-permute-start.2
  37.4 4.0 %collective-permute-start.26 = (f32[3,16,4,1]{3,1,2,0:T(8,128)S(1)}, f32[3,16,4,1]{3,1,2,0:T(8,128)S(1)}, u32[]{:S(2)}, u32[]{:S(2)}) collective-permute-start(f32[3,16,4,1]{3,1,2,0:T(8,128)S(1)} %get-tuple-element.948), channel_id=1, source_target_pairs={{0,2},{1,3},{4,6},{5,7},{8,10},{9,11},{12,14},{13,15},{16,18},{17,... | collective-permute-start | bytes 2312 | tf_op jit(solution)/shard_map/ppermute | solution.py:21
  42.9 4.0 %collective-permute-start.50 = (f32[3,16,4,1]{3,1,2,0:T(8,128)S(1)}, f32[3,16,4,1]{3,1,2,0:T(8,128)S(1)}, u32[]{:S(2)}, u32[]{:S(2)}) collective-permute-start(f32[3,16,4,1]{3,1,2,0:T(8,128)S(1)} %get-tuple-element.952), channel_id=1, source_target_pairs={{0,2},{1,3},{4,6},{5,7},{8,10},{9,11},{12,14},{13,15},{16,18},{17,... | collective-permute-start | bytes 2312 | tf_op jit(solution)/shard_map/ppermute | solution.py:21
  48.3 4.0 %collective-permute-start.74 = (f32[3,16,4,1]{3,1,2,0:T(8,128)S(1)}, f32[3,16,4,1]{3,1,2,0:T(8,128)S(1)}, u32[]{:S(2)}, u32[]{:S(2)}) collective-permute-start(f32[3,16,4,1]{3,1,2,0:T(8,128)S(1)} %get-tuple-element.956), channel_id=1, source_target_pairs={{0,2},{1,3},{4,6},{5,7},{8,10},{9,11},{12,14},{13,15},{16,18},{17,... | collective-permute-start | bytes 2312 | tf_op jit(solution)/shard_map/ppermute | solution.py:21
  54.5 4.3 %collective-permute-done.75 = f32[3,16,4,1]{3,1,2,0:T(8,128)S(1)} collective-permute-done((f32[3,16,4,1]{3,1,2,0:T(8,128)S(1)}, f32[3,16,4,1]{3,1,2,0:T(8,128)S(1)}, u32[]{:S(2)}, u32[]{:S(2)}) %collective-permute-start.75) | collective-permute-done | bytes 800 | tf_op jit(solution)/shard_map/ppermute | solution.py:22
  59.3 7.6 %collective-permute-start.4 = (f32[3,1,4,130]{3,1,2,0:T(1,128)S(1)}, f32[3,1,4,130]{3,1,2,0:T(1,128)S(1)}, u32[]{:S(2)}, u32[]{:S(2)}) collective-permute-start(f32[3,1,4,130]{3,1,2,0:T(1,128)S(1)} %get-tuple-element.800), channel_id=1, source_target_pairs={{1,0},{3,2},{5,4},{7,6},{9,8},{11,10},{13,12},{15,14},{17,16},{19,... | collective-permute-start | bytes 18728 | tf_op jit(solution)/shard_map/ppermute | solution.py:22
  68.5 3.0 collective-permute-start.28
  73.2 3.0 collective-permute-start.52
  78.4 3.0 collective-permute-start.76
  81.6 1.3 collective-permute-start.77
  82.9 4.3 %collective-permute-start.6 = (f32[3,16,1,128]{3,1,2,0:T(8,128)S(1)}, f32[3,16,1,128]{3,1,2,0:T(8,128)S(1)}, u32[]{:S(2)}, u32[]{:S(2)}) collective-permute-start(f32[3,16,1,128]{3,1,2,0:T(8,128)S(1)} %get-tuple-element.1051), channel_id=1, source_target_pairs={{0,4},{4,8},{8,12},{1,5},{5,9},{9,13},{2,6},{6,10},{10,14},{3,7},{... | collective-permute-start | bytes 73736 | tf_op jit(solution)/shard_map/ppermute | solution.py:21
  88.6 4.0 %collective-permute-start.30 = (f32[3,16,1,128]{3,1,2,0:T(8,128)S(1)}, f32[3,16,1,128]{3,1,2,0:T(8,128)S(1)}, u32[]{:S(2)}, u32[]{:S(2)}) collective-permute-start(f32[3,16,1,128]{3,1,2,0:T(8,128)S(1)} %get-tuple-element.1055), channel_id=1, source_target_pairs={{0,4},{4,8},{8,12},{1,5},{5,9},{9,13},{2,6},{6,10},{10,14},{3,7},{... | collective-permute-start | bytes 73736 | tf_op jit(solution)/shard_map/ppermute | solution.py:21
  94.1 4.0 %collective-permute-start.54 = (f32[3,16,1,128]{3,1,2,0:T(8,128)S(1)}, f32[3,16,1,128]{3,1,2,0:T(8,128)S(1)}, u32[]{:S(2)}, u32[]{:S(2)}) collective-permute-start(f32[3,16,1,128]{3,1,2,0:T(8,128)S(1)} %get-tuple-element.1059), channel_id=1, source_target_pairs={{0,4},{4,8},{8,12},{1,5},{5,9},{9,13},{2,6},{6,10},{10,14},{3,7},{... | collective-permute-start | bytes 73736 | tf_op jit(solution)/shard_map/ppermute | solution.py:21
  99.5 4.0 %collective-permute-start.78 = (f32[3,16,1,128]{3,1,2,0:T(8,128)S(1)}, f32[3,16,1,128]{3,1,2,0:T(8,128)S(1)}, u32[]{:S(2)}, u32[]{:S(2)}) collective-permute-start(f32[3,16,1,128]{3,1,2,0:T(8,128)S(1)} %get-tuple-element.1063), channel_id=1, source_target_pairs={{0,4},{4,8},{8,12},{1,5},{5,9},{9,13},{2,6},{6,10},{10,14},{3,7},{... | collective-permute-start | bytes 73736 | tf_op jit(solution)/shard_map/ppermute | solution.py:21
  104.9 1.3 collective-permute-start.8
  107.7 4.0 %collective-permute-start.32 = (f32[3,16,4,1]{3,1,2,0:T(8,128)S(1)}, f32[3,16,4,1]{3,1,2,0:T(8,128)S(1)}, u32[]{:S(2)}, u32[]{:S(2)}) collective-permute-start(f32[3,16,4,1]{3,1,2,0:T(8,128)S(1)} %get-tuple-element.946), channel_id=1, source_target_pairs={{0,2},{1,3},{4,6},{5,7},{8,10},{9,11},{12,14},{13,15},{16,18},{17,... | collective-permute-start | bytes 2312 | tf_op jit(solution)/shard_map/ppermute | solution.py:21
  113.1 4.0 %collective-permute-start.56 = (f32[3,16,4,1]{3,1,2,0:T(8,128)S(1)}, f32[3,16,4,1]{3,1,2,0:T(8,128)S(1)}, u32[]{:S(2)}, u32[]{:S(2)}) collective-permute-start(f32[3,16,4,1]{3,1,2,0:T(8,128)S(1)} %get-tuple-element.950), channel_id=1, source_target_pairs={{0,2},{1,3},{4,6},{5,7},{8,10},{9,11},{12,14},{13,15},{16,18},{17,... | collective-permute-start | bytes 2312 | tf_op jit(solution)/shard_map/ppermute | solution.py:21
  118.5 4.0 %collective-permute-start.80 = (f32[3,16,4,1]{3,1,2,0:T(8,128)S(1)}, f32[3,16,4,1]{3,1,2,0:T(8,128)S(1)}, u32[]{:S(2)}, u32[]{:S(2)}) collective-permute-start(f32[3,16,4,1]{3,1,2,0:T(8,128)S(1)} %get-tuple-element.954), channel_id=1, source_target_pairs={{0,2},{1,3},{4,6},{5,7},{8,10},{9,11},{12,14},{13,15},{16,18},{17,... | collective-permute-start | bytes 2312 | tf_op jit(solution)/shard_map/ppermute | solution.py:21
  124.5 4.1 %collective-permute-done.81 = f32[3,16,4,1]{3,1,2,0:T(8,128)S(1)} collective-permute-done((f32[3,16,4,1]{3,1,2,0:T(8,128)S(1)}, f32[3,16,4,1]{3,1,2,0:T(8,128)S(1)}, u32[]{:S(2)}, u32[]{:S(2)}) %collective-permute-start.81) | collective-permute-done | bytes 800 | tf_op jit(solution)/shard_map/ppermute | solution.py:22
  129.1 7.6 %collective-permute-start.10 = (f32[3,1,4,130]{3,1,2,0:T(1,128)S(1)}, f32[3,1,4,130]{3,1,2,0:T(1,128)S(1)}, u32[]{:S(2)}, u32[]{:S(2)}) collective-permute-start(f32[3,1,4,130]{3,1,2,0:T(1,128)S(1)} %get-tuple-element.798), channel_id=1, source_target_pairs={{1,0},{3,2},{5,4},{7,6},{9,8},{11,10},{13,12},{15,14},{17,16},{19,... | collective-permute-start | bytes 18728 | tf_op jit(solution)/shard_map/ppermute | solution.py:22
  136.8 1.3 collective-permute-start.11
  138.4 3.0 collective-permute-start.34
  143.1 3.0 collective-permute-start.58
  147.4 1.3 collective-permute-start.59
  148.7 3.0 collective-permute-start.82
  151.8 1.3 collective-permute-start.83
  153.2 1.6 collective-permute-done.83
  159.2 2.1 collective-permute-start.12
  161.3 4.3 %collective-permute-start.17 = (f32[3,16,2]{1,2,0:T(2,128)S(1)}, f32[3,16,2]{1,2,0:T(2,128)S(1)}, u32[]{:S(2)}, u32[]{:S(2)}) collective-permute-start(f32[3,16,2]{1,2,0:T(2,128)S(1)} %get-tuple-element.662), channel_id=1, source_target_pairs={{0,2},{1,3},{4,6},{5,7},{8,10},{9,11},{12,14},{13,15},{16,18},{17,... | collective-permute-start | bytes 1160 | tf_op jit(solution)/shard_map/ppermute | solution.py:30
  167.1 4.9 %collective-permute-start.15 = (f32[3,16,128]{2,1,0:T(8,128)S(1)}, f32[3,16,128]{2,1,0:T(8,128)S(1)}, u32[]{:S(2)}, u32[]{:S(2)}) collective-permute-start(f32[3,16,128]{2,1,0:T(8,128)S(1)} %get-tuple-element.794), channel_id=1, source_target_pairs={{0,4},{4,8},{8,12},{1,5},{5,9},{9,13},{2,6},{6,10},{10,14},{3,7},{... | collective-permute-start | bytes 73736 | tf_op jit(solution)/shard_map/ppermute | solution.py:30
  175.0 3.9 %collective-permute-start.18 = (f32[3,2,128]{2,1,0:T(2,128)S(1)}, f32[3,2,128]{2,1,0:T(2,128)S(1)}, u32[]{:S(2)}, u32[]{:S(2)}) collective-permute-start(f32[3,2,128]{2,1,0:T(2,128)S(1)} %bitcast.1241), channel_id=1, source_target_pairs={{1,0},{3,2},{5,4},{7,6},{9,8},{11,10},{13,12},{15,14},{17,16},{19,... | collective-permute-start | bytes 9224 | tf_op jit(solution)/shard_map/ppermute | solution.py:30
  179.1 1.3 collective-permute-start.22
  180.4 1.3 collective-permute-start.20
  181.8 4.0 %collective-permute-start.23 = (f32[3,16,2]{1,2,0:T(2,128)S(1)}, f32[3,16,2]{1,2,0:T(2,128)S(1)}, u32[]{:S(2)}, u32[]{:S(2)}) collective-permute-start(f32[3,16,2]{1,2,0:T(2,128)S(1)} %get-tuple-element.660), channel_id=1, source_target_pairs={{0,2},{1,3},{4,6},{5,7},{8,10},{9,11},{12,14},{13,15},{16,18},{17,... | collective-permute-start | bytes 1160 | tf_op jit(solution)/shard_map/ppermute | solution.py:30
  187.1 4.6 %collective-permute-start.21 = (f32[3,16,128]{2,1,0:T(8,128)S(1)}, f32[3,16,128]{2,1,0:T(8,128)S(1)}, u32[]{:S(2)}, u32[]{:S(2)}) collective-permute-start(f32[3,16,128]{2,1,0:T(8,128)S(1)} %get-tuple-element.789), channel_id=1, source_target_pairs={{0,4},{4,8},{8,12},{1,5},{5,9},{9,13},{2,6},{6,10},{10,14},{3,7},{... | collective-permute-start | bytes 73736 | tf_op jit(solution)/shard_map/ppermute | solution.py:30
  194.5 3.9 %collective-permute-start.36 = (f32[3,2,128]{2,1,0:T(2,128)S(1)}, f32[3,2,128]{2,1,0:T(2,128)S(1)}, u32[]{:S(2)}, u32[]{:S(2)}) collective-permute-start(f32[3,2,128]{2,1,0:T(2,128)S(1)} %bitcast.1268), channel_id=1, source_target_pairs={{1,0},{3,2},{5,4},{7,6},{9,8},{11,10},{13,12},{15,14},{17,16},{19,... | collective-permute-start | bytes 9224 | tf_op jit(solution)/shard_map/ppermute | solution.py:30
  199.9 1.3 collective-permute-start.37
  201.3 4.0 %collective-permute-start.41 = (f32[3,16,2]{1,2,0:T(2,128)S(1)}, f32[3,16,2]{1,2,0:T(2,128)S(1)}, u32[]{:S(2)}, u32[]{:S(2)}) collective-permute-start(f32[3,16,2]{1,2,0:T(2,128)S(1)} %bitcast.1257), channel_id=1, source_target_pairs={{0,2},{1,3},{4,6},{5,7},{8,10},{9,11},{12,14},{13,15},{16,18},{17,... | collective-permute-start | bytes 1160 | tf_op jit(solution)/shard_map/ppermute | solution.py:30
  206.6 4.6 %collective-permute-start.39 = (f32[3,16,128]{2,1,0:T(8,128)S(1)}, f32[3,16,128]{2,1,0:T(8,128)S(1)}, u32[]{:S(2)}, u32[]{:S(2)}) collective-permute-start(f32[3,16,128]{2,1,0:T(8,128)S(1)} %get-tuple-element.785), channel_id=1, source_target_pairs={{0,4},{4,8},{8,12},{1,5},{5,9},{9,13},{2,6},{6,10},{10,14},{3,7},{... | collective-permute-start | bytes 73736 | tf_op jit(solution)/shard_map/ppermute | solution.py:30
  214.0 4.2 %collective-permute-start.42 = (f32[3,2,128]{2,1,0:T(2,128)S(1)}, f32[3,2,128]{2,1,0:T(2,128)S(1)}, u32[]{:S(2)}, u32[]{:S(2)}) collective-permute-start(f32[3,2,128]{2,1,0:T(2,128)S(1)} %bitcast.1242), channel_id=1, source_target_pairs={{1,0},{3,2},{5,4},{7,6},{9,8},{11,10},{13,12},{15,14},{17,16},{19,... | collective-permute-start | bytes 9224 | tf_op jit(solution)/shard_map/ppermute | solution.py:30
  221.1 4.0 %collective-permute-start.47 = (f32[3,16,2]{1,2,0:T(2,128)S(1)}, f32[3,16,2]{1,2,0:T(2,128)S(1)}, u32[]{:S(2)}, u32[]{:S(2)}) collective-permute-start(f32[3,16,2]{1,2,0:T(2,128)S(1)} %get-tuple-element.658), channel_id=1, source_target_pairs={{0,2},{1,3},{4,6},{5,7},{8,10},{9,11},{12,14},{13,15},{16,18},{17,... | collective-permute-start | bytes 1160 | tf_op jit(solution)/shard_map/ppermute | solution.py:30
  226.4 4.6 %collective-permute-start.45 = (f32[3,16,128]{2,1,0:T(8,128)S(1)}, f32[3,16,128]{2,1,0:T(8,128)S(1)}, u32[]{:S(2)}, u32[]{:S(2)}) collective-permute-start(f32[3,16,128]{2,1,0:T(8,128)S(1)} %get-tuple-element.778), channel_id=1, source_target_pairs={{0,4},{4,8},{8,12},{1,5},{5,9},{9,13},{2,6},{6,10},{10,14},{3,7},{... | collective-permute-start | bytes 73736 | tf_op jit(solution)/shard_map/ppermute | solution.py:30
  233.8 3.9 %collective-permute-start.60 = (f32[3,2,128]{2,1,0:T(2,128)S(1)}, f32[3,2,128]{2,1,0:T(2,128)S(1)}, u32[]{:S(2)}, u32[]{:S(2)}) collective-permute-start(f32[3,2,128]{2,1,0:T(2,128)S(1)} %bitcast.1269), channel_id=1, source_target_pairs={{1,0},{3,2},{5,4},{7,6},{9,8},{11,10},{13,12},{15,14},{17,16},{19,... | collective-permute-start | bytes 9224 | tf_op jit(solution)/shard_map/ppermute | solution.py:30
  240.6 4.0 %collective-permute-start.65 = (f32[3,16,2]{1,2,0:T(2,128)S(1)}, f32[3,16,2]{1,2,0:T(2,128)S(1)}, u32[]{:S(2)}, u32[]{:S(2)}) collective-permute-start(f32[3,16,2]{1,2,0:T(2,128)S(1)} %bitcast.1261), channel_id=1, source_target_pairs={{0,2},{1,3},{4,6},{5,7},{8,10},{9,11},{12,14},{13,15},{16,18},{17,... | collective-permute-start | bytes 1160 | tf_op jit(solution)/shard_map/ppermute | solution.py:30
  245.9 4.6 %collective-permute-start.63 = (f32[3,16,128]{2,1,0:T(8,128)S(1)}, f32[3,16,128]{2,1,0:T(8,128)S(1)}, u32[]{:S(2)}, u32[]{:S(2)}) collective-permute-start(f32[3,16,128]{2,1,0:T(8,128)S(1)} %get-tuple-element.774), channel_id=1, source_target_pairs={{0,4},{4,8},{8,12},{1,5},{5,9},{9,13},{2,6},{6,10},{10,14},{3,7},{... | collective-permute-start | bytes 73736 | tf_op jit(solution)/shard_map/ppermute | solution.py:30
  253.3 4.2 %collective-permute-start.66 = (f32[3,2,128]{2,1,0:T(2,128)S(1)}, f32[3,2,128]{2,1,0:T(2,128)S(1)}, u32[]{:S(2)}, u32[]{:S(2)}) collective-permute-start(f32[3,2,128]{2,1,0:T(2,128)S(1)} %bitcast.1243), channel_id=1, source_target_pairs={{1,0},{3,2},{5,4},{7,6},{9,8},{11,10},{13,12},{15,14},{17,16},{19,... | collective-permute-start | bytes 9224 | tf_op jit(solution)/shard_map/ppermute | solution.py:30
  260.3 4.0 %collective-permute-start.71 = (f32[3,16,2]{1,2,0:T(2,128)S(1)}, f32[3,16,2]{1,2,0:T(2,128)S(1)}, u32[]{:S(2)}, u32[]{:S(2)}) collective-permute-start(f32[3,16,2]{1,2,0:T(2,128)S(1)} %get-tuple-element.656), channel_id=1, source_target_pairs={{0,2},{1,3},{4,6},{5,7},{8,10},{9,11},{12,14},{13,15},{16,18},{17,... | collective-permute-start | bytes 1160 | tf_op jit(solution)/shard_map/ppermute | solution.py:30
  265.6 4.6 %collective-permute-start.69 = (f32[3,16,128]{2,1,0:T(8,128)S(1)}, f32[3,16,128]{2,1,0:T(8,128)S(1)}, u32[]{:S(2)}, u32[]{:S(2)}) collective-permute-start(f32[3,16,128]{2,1,0:T(8,128)S(1)} %get-tuple-element.767), channel_id=1, source_target_pairs={{0,4},{4,8},{8,12},{1,5},{5,9},{9,13},{2,6},{6,10},{10,14},{3,7},{... | collective-permute-start | bytes 73736 | tf_op jit(solution)/shard_map/ppermute | solution.py:30
  273.0 3.9 %collective-permute-start.84 = (f32[3,2,128]{2,1,0:T(2,128)S(1)}, f32[3,2,128]{2,1,0:T(2,128)S(1)}, u32[]{:S(2)}, u32[]{:S(2)}) collective-permute-start(f32[3,2,128]{2,1,0:T(2,128)S(1)} %bitcast.1270), channel_id=1, source_target_pairs={{1,0},{3,2},{5,4},{7,6},{9,8},{11,10},{13,12},{15,14},{17,16},{19,... | collective-permute-start | bytes 9224 | tf_op jit(solution)/shard_map/ppermute | solution.py:30
  279.9 4.0 %collective-permute-start.89 = (f32[3,16,2]{1,2,0:T(2,128)S(1)}, f32[3,16,2]{1,2,0:T(2,128)S(1)}, u32[]{:S(2)}, u32[]{:S(2)}) collective-permute-start(f32[3,16,2]{1,2,0:T(2,128)S(1)} %bitcast.1265), channel_id=1, source_target_pairs={{0,2},{1,3},{4,6},{5,7},{8,10},{9,11},{12,14},{13,15},{16,18},{17,... | collective-permute-start | bytes 1160 | tf_op jit(solution)/shard_map/ppermute | solution.py:30
  285.2 4.6 %collective-permute-start.87 = (f32[3,16,128]{2,1,0:T(8,128)S(1)}, f32[3,16,128]{2,1,0:T(8,128)S(1)}, u32[]{:S(2)}, u32[]{:S(2)}) collective-permute-start(f32[3,16,128]{2,1,0:T(8,128)S(1)} %get-tuple-element.763), channel_id=1, source_target_pairs={{0,4},{4,8},{8,12},{1,5},{5,9},{9,13},{2,6},{6,10},{10,14},{3,7},{... | collective-permute-start | bytes 73736 | tf_op jit(solution)/shard_map/ppermute | solution.py:30
  292.6 17.1 %all-reduce.312 = (f32[16]{0:T(128)S(1)}, f32[16]{0:T(128)S(1)}) all-reduce(f32[16]{0:T(128)S(1)} %add_multiply_fusion, f32[16]{0:T(128)S(1)} %add_add_fusion.1), channel_id=1, replica_groups=mesh['ens'=2,'gx'=4,'col'=2,'gz'=2] {'gx','col'}, use_global_device_ids=true, to_apply=%region_1.0 | all-reduce | flops 32 | bytes 256 | tf_op jit(solution)/shard_map/psum | solution.py:146
  310.7 8.2 %collective-permute-start.90 = (f32[3,2,128]{2,1,0:T(2,128)S(1)}, f32[3,2,128]{2,1,0:T(2,128)S(1)}, u32[]{:S(2)}, u32[]{:S(2)}) collective-permute-start(f32[3,2,128]{2,1,0:T(2,128)S(1)} %bitcast.1236), channel_id=1, source_target_pairs={{1,0},{3,2},{5,4},{7,6},{9,8},{11,10},{13,12},{15,14},{17,16},{19,... | collective-permute-start | bytes 9224 | tf_op jit(solution)/shard_map/ppermute | solution.py:30
  319.1 1.3 collective-permute-start.94
  321.8 4.0 %collective-permute-start.95 = (f32[3,16,2]{1,2,0:T(2,128)S(1)}, f32[3,16,2]{1,2,0:T(2,128)S(1)}, u32[]{:S(2)}, u32[]{:S(2)}) collective-permute-start(f32[3,16,2]{1,2,0:T(2,128)S(1)} %get-tuple-element.654), channel_id=1, source_target_pairs={{0,2},{1,3},{4,6},{5,7},{8,10},{9,11},{12,14},{13,15},{16,18},{17,... | collective-permute-start | bytes 1160 | tf_op jit(solution)/shard_map/ppermute | solution.py:30
  327.1 4.0 %collective-permute-start.93 = (f32[3,16,128]{2,1,0:T(8,128)S(1)}, f32[3,16,128]{2,1,0:T(8,128)S(1)}, u32[]{:S(2)}, u32[]{:S(2)}) collective-permute-start(f32[3,16,128]{2,1,0:T(8,128)S(1)} %get-tuple-element.756), channel_id=1, source_target_pairs={{0,4},{4,8},{8,12},{1,5},{5,9},{9,13},{2,6},{6,10},{10,14},{3,7},{... | collective-permute-start | bytes 73736 | tf_op jit(solution)/shard_map/ppermute | solution.py:30
  (484 shorter events, 88.3 us)
Async XLA Ops:
  13.2 14.1 %collective-permute-start = (f32[3,16,1,128]{3,1,2,0:T(8,128)S(1)}, f32[3,16,1,128]{3,1,2,0:T(8,128)S(1)}, u32[]{:S(2)}, u32[]{:S(2)}) collective-permute-start(f32[3,16,1,128]{3,1,2,0:T(8,128)S(1)} %get-tuple-element.1053), channel_id=1, source_target_pairs={{0,4},{4,8},{8,12},{1,5},{5,9},{9,13},{2,6},{6,10},{10,14},{3,7},{... | collective-permute-start | bytes 73736 | tf_op jit(solution)/shard_map/ppermute | solution.py:21
  16.6 11.9 %collective-permute-start.1 = (f32[3,16,1,128]{3,1,2,0:T(8,128)S(1)}, f32[3,16,1,128]{3,1,2,0:T(8,128)S(1)}, u32[]{:S(2)}, u32[]{:S(2)}) collective-permute-start(f32[3,16,1,128]{3,1,2,0:T(8,128)S(1)} %get-tuple-element.1054), channel_id=1, source_target_pairs={{4,0},{8,4},{12,8},{5,1},{9,5},{13,9},{6,2},{10,6},{14,10},{7,3},{... | collective-permute-start | bytes 73736 | tf_op jit(solution)/shard_map/ppermute | solution.py:22
  17.9 14.7 %collective-permute-start.24 = (f32[3,16,1,128]{3,1,2,0:T(8,128)S(1)}, f32[3,16,1,128]{3,1,2,0:T(8,128)S(1)}, u32[]{:S(2)}, u32[]{:S(2)}) collective-permute-start(f32[3,16,1,128]{3,1,2,0:T(8,128)S(1)} %get-tuple-element.1057), channel_id=1, source_target_pairs={{0,4},{4,8},{8,12},{1,5},{5,9},{9,13},{2,6},{6,10},{10,14},{3,7},{... | collective-permute-start | bytes 73736 | tf_op jit(solution)/shard_map/ppermute | solution.py:21
  21.9 12.1 %collective-permute-start.25 = (f32[3,16,1,128]{3,1,2,0:T(8,128)S(1)}, f32[3,16,1,128]{3,1,2,0:T(8,128)S(1)}, u32[]{:S(2)}, u32[]{:S(2)}) collective-permute-start(f32[3,16,1,128]{3,1,2,0:T(8,128)S(1)} %get-tuple-element.1058), channel_id=1, source_target_pairs={{4,0},{8,4},{12,8},{5,1},{9,5},{13,9},{6,2},{10,6},{14,10},{7,3},{... | collective-permute-start | bytes 73736 | tf_op jit(solution)/shard_map/ppermute | solution.py:22
  23.2 12.9 %collective-permute-start.48 = (f32[3,16,1,128]{3,1,2,0:T(8,128)S(1)}, f32[3,16,1,128]{3,1,2,0:T(8,128)S(1)}, u32[]{:S(2)}, u32[]{:S(2)}) collective-permute-start(f32[3,16,1,128]{3,1,2,0:T(8,128)S(1)} %get-tuple-element.1061), channel_id=1, source_target_pairs={{0,4},{4,8},{8,12},{1,5},{5,9},{9,13},{2,6},{6,10},{10,14},{3,7},{... | collective-permute-start | bytes 73736 | tf_op jit(solution)/shard_map/ppermute | solution.py:21
  27.3 10.2 %collective-permute-start.49 = (f32[3,16,1,128]{3,1,2,0:T(8,128)S(1)}, f32[3,16,1,128]{3,1,2,0:T(8,128)S(1)}, u32[]{:S(2)}, u32[]{:S(2)}) collective-permute-start(f32[3,16,1,128]{3,1,2,0:T(8,128)S(1)} %get-tuple-element.1062), channel_id=1, source_target_pairs={{4,0},{8,4},{12,8},{5,1},{9,5},{13,9},{6,2},{10,6},{14,10},{7,3},{... | collective-permute-start | bytes 73736 | tf_op jit(solution)/shard_map/ppermute | solution.py:22
  28.6 13.0 %collective-permute-start.72 = (f32[3,16,1,128]{3,1,2,0:T(8,128)S(1)}, f32[3,16,1,128]{3,1,2,0:T(8,128)S(1)}, u32[]{:S(2)}, u32[]{:S(2)}) collective-permute-start(f32[3,16,1,128]{3,1,2,0:T(8,128)S(1)} %get-tuple-element.1065), channel_id=1, source_target_pairs={{0,4},{4,8},{8,12},{1,5},{5,9},{9,13},{2,6},{6,10},{10,14},{3,7},{... | collective-permute-start | bytes 73736 | tf_op jit(solution)/shard_map/ppermute | solution.py:21
  32.7 10.2 %collective-permute-start.73 = (f32[3,16,1,128]{3,1,2,0:T(8,128)S(1)}, f32[3,16,1,128]{3,1,2,0:T(8,128)S(1)}, u32[]{:S(2)}, u32[]{:S(2)}) collective-permute-start(f32[3,16,1,128]{3,1,2,0:T(8,128)S(1)} %get-tuple-element.1066), channel_id=1, source_target_pairs={{4,0},{8,4},{12,8},{5,1},{9,5},{13,9},{6,2},{10,6},{14,10},{7,3},{... | collective-permute-start | bytes 73736 | tf_op jit(solution)/shard_map/ppermute | solution.py:22
  34.0 13.0 %collective-permute-start.2 = (f32[3,16,4,1]{3,1,2,0:T(8,128)S(1)}, f32[3,16,4,1]{3,1,2,0:T(8,128)S(1)}, u32[]{:S(2)}, u32[]{:S(2)}) collective-permute-start(f32[3,16,4,1]{3,1,2,0:T(8,128)S(1)} %get-tuple-element.944), channel_id=1, source_target_pairs={{0,2},{1,3},{4,6},{5,7},{8,10},{9,11},{12,14},{13,15},{16,18},{17,... | collective-permute-start | bytes 2312 | tf_op jit(solution)/shard_map/ppermute | solution.py:21
  36.1 12.2 %collective-permute-start.3 = (f32[3,16,4,1]{3,1,2,0:T(8,128)S(1)}, f32[3,16,4,1]{3,1,2,0:T(8,128)S(1)}, u32[]{:S(2)}, u32[]{:S(2)}) collective-permute-start(f32[3,16,4,1]{3,1,2,0:T(8,128)S(1)} %get-tuple-element.945), channel_id=1, source_target_pairs={{2,0},{3,1},{6,4},{7,5},{10,8},{11,9},{14,12},{15,13},{18,16},{19,... | collective-permute-start | bytes 2312 | tf_op jit(solution)/shard_map/ppermute | solution.py:22
  37.4 15.1 %collective-permute-start.26 = (f32[3,16,4,1]{3,1,2,0:T(8,128)S(1)}, f32[3,16,4,1]{3,1,2,0:T(8,128)S(1)}, u32[]{:S(2)}, u32[]{:S(2)}) collective-permute-start(f32[3,16,4,1]{3,1,2,0:T(8,128)S(1)} %get-tuple-element.948), channel_id=1, source_target_pairs={{0,2},{1,3},{4,6},{5,7},{8,10},{9,11},{12,14},{13,15},{16,18},{17,... | collective-permute-start | bytes 2312 | tf_op jit(solution)/shard_map/ppermute | solution.py:21
  41.5 12.2 %collective-permute-start.27 = (f32[3,16,4,1]{3,1,2,0:T(8,128)S(1)}, f32[3,16,4,1]{3,1,2,0:T(8,128)S(1)}, u32[]{:S(2)}, u32[]{:S(2)}) collective-permute-start(f32[3,16,4,1]{3,1,2,0:T(8,128)S(1)} %get-tuple-element.949), channel_id=1, source_target_pairs={{2,0},{3,1},{6,4},{7,5},{10,8},{11,9},{14,12},{15,13},{18,16},{19,... | collective-permute-start | bytes 2312 | tf_op jit(solution)/shard_map/ppermute | solution.py:22
  42.9 11.1 %collective-permute-start.50 = (f32[3,16,4,1]{3,1,2,0:T(8,128)S(1)}, f32[3,16,4,1]{3,1,2,0:T(8,128)S(1)}, u32[]{:S(2)}, u32[]{:S(2)}) collective-permute-start(f32[3,16,4,1]{3,1,2,0:T(8,128)S(1)} %get-tuple-element.952), channel_id=1, source_target_pairs={{0,2},{1,3},{4,6},{5,7},{8,10},{9,11},{12,14},{13,15},{16,18},{17,... | collective-permute-start | bytes 2312 | tf_op jit(solution)/shard_map/ppermute | solution.py:21
  59.3 17.8 %collective-permute-start.4 = (f32[3,1,4,130]{3,1,2,0:T(1,128)S(1)}, f32[3,1,4,130]{3,1,2,0:T(1,128)S(1)}, u32[]{:S(2)}, u32[]{:S(2)}) collective-permute-start(f32[3,1,4,130]{3,1,2,0:T(1,128)S(1)} %get-tuple-element.800), channel_id=1, source_target_pairs={{1,0},{3,2},{5,4},{7,6},{9,8},{11,10},{13,12},{15,14},{17,16},{19,... | collective-permute-start | bytes 18728 | tf_op jit(solution)/shard_map/ppermute | solution.py:22
  66.9 11.5 %collective-permute-start.5 = (f32[3,1,4,130]{3,1,2,0:T(1,128)S(1)}, f32[3,1,4,130]{3,1,2,0:T(1,128)S(1)}, u32[]{:S(2)}, u32[]{:S(2)}) collective-permute-start(f32[3,1,4,130]{3,1,2,0:T(1,128)S(1)} %get-tuple-element.801), channel_id=1, source_target_pairs={{0,1},{2,3},{4,5},{6,7},{8,9},{10,11},{12,13},{14,15},{16,17},{18,... | collective-permute-start | bytes 18728 | tf_op jit(solution)/shard_map/ppermute | solution.py:21
  68.5 13.1 %collective-permute-start.28 = (f32[3,1,4,130]{3,1,2,0:T(1,128)S(1)}, f32[3,1,4,130]{3,1,2,0:T(1,128)S(1)}, u32[]{:S(2)}, u32[]{:S(2)}) collective-permute-start(f32[3,1,4,130]{3,1,2,0:T(1,128)S(1)} %get-tuple-element.804), channel_id=1, source_target_pairs={{1,0},{3,2},{5,4},{7,6},{9,8},{11,10},{13,12},{15,14},{17,16},{19,... | collective-permute-start | bytes 18728 | tf_op jit(solution)/shard_map/ppermute | solution.py:22
  71.6 11.3 %collective-permute-start.29 = (f32[3,1,4,130]{3,1,2,0:T(1,128)S(1)}, f32[3,1,4,130]{3,1,2,0:T(1,128)S(1)}, u32[]{:S(2)}, u32[]{:S(2)}) collective-permute-start(f32[3,1,4,130]{3,1,2,0:T(1,128)S(1)} %get-tuple-element.805), channel_id=1, source_target_pairs={{0,1},{2,3},{4,5},{6,7},{8,9},{10,11},{12,13},{14,15},{16,17},{18,... | collective-permute-start | bytes 18728 | tf_op jit(solution)/shard_map/ppermute | solution.py:21
  73.2 14.1 %collective-permute-start.52 = (f32[3,1,4,130]{3,1,2,0:T(1,128)S(1)}, f32[3,1,4,130]{3,1,2,0:T(1,128)S(1)}, u32[]{:S(2)}, u32[]{:S(2)}) collective-permute-start(f32[3,1,4,130]{3,1,2,0:T(1,128)S(1)} %get-tuple-element.808), channel_id=1, source_target_pairs={{1,0},{3,2},{5,4},{7,6},{9,8},{11,10},{13,12},{15,14},{17,16},{19,... | collective-permute-start | bytes 18728 | tf_op jit(solution)/shard_map/ppermute | solution.py:22
  77.1 11.5 %collective-permute-start.53 = (f32[3,1,4,130]{3,1,2,0:T(1,128)S(1)}, f32[3,1,4,130]{3,1,2,0:T(1,128)S(1)}, u32[]{:S(2)}, u32[]{:S(2)}) collective-permute-start(f32[3,1,4,130]{3,1,2,0:T(1,128)S(1)} %get-tuple-element.809), channel_id=1, source_target_pairs={{0,1},{2,3},{4,5},{6,7},{8,9},{10,11},{12,13},{14,15},{16,17},{18,... | collective-permute-start | bytes 18728 | tf_op jit(solution)/shard_map/ppermute | solution.py:21
  78.4 14.3 %collective-permute-start.76 = (f32[3,1,4,130]{3,1,2,0:T(1,128)S(1)}, f32[3,1,4,130]{3,1,2,0:T(1,128)S(1)}, u32[]{:S(2)}, u32[]{:S(2)}) collective-permute-start(f32[3,1,4,130]{3,1,2,0:T(1,128)S(1)} %get-tuple-element.812), channel_id=1, source_target_pairs={{1,0},{3,2},{5,4},{7,6},{9,8},{11,10},{13,12},{15,14},{17,16},{19,... | collective-permute-start | bytes 18728 | tf_op jit(solution)/shard_map/ppermute | solution.py:22
  81.6 12.5 %collective-permute-start.77 = (f32[3,1,4,130]{3,1,2,0:T(1,128)S(1)}, f32[3,1,4,130]{3,1,2,0:T(1,128)S(1)}, u32[]{:S(2)}, u32[]{:S(2)}) collective-permute-start(f32[3,1,4,130]{3,1,2,0:T(1,128)S(1)} %get-tuple-element.813), channel_id=1, source_target_pairs={{0,1},{2,3},{4,5},{6,7},{8,9},{10,11},{12,13},{14,15},{16,17},{18,... | collective-permute-start | bytes 18728 | tf_op jit(solution)/shard_map/ppermute | solution.py:21
  82.9 15.3 %collective-permute-start.6 = (f32[3,16,1,128]{3,1,2,0:T(8,128)S(1)}, f32[3,16,1,128]{3,1,2,0:T(8,128)S(1)}, u32[]{:S(2)}, u32[]{:S(2)}) collective-permute-start(f32[3,16,1,128]{3,1,2,0:T(8,128)S(1)} %get-tuple-element.1051), channel_id=1, source_target_pairs={{0,4},{4,8},{8,12},{1,5},{5,9},{9,13},{2,6},{6,10},{10,14},{3,7},{... | collective-permute-start | bytes 73736 | tf_op jit(solution)/shard_map/ppermute | solution.py:21
  87.3 12.2 %collective-permute-start.7 = (f32[3,16,1,128]{3,1,2,0:T(8,128)S(1)}, f32[3,16,1,128]{3,1,2,0:T(8,128)S(1)}, u32[]{:S(2)}, u32[]{:S(2)}) collective-permute-start(f32[3,16,1,128]{3,1,2,0:T(8,128)S(1)} %get-tuple-element.1052), channel_id=1, source_target_pairs={{4,0},{8,4},{12,8},{5,1},{9,5},{13,9},{6,2},{10,6},{14,10},{7,3},{... | collective-permute-start | bytes 73736 | tf_op jit(solution)/shard_map/ppermute | solution.py:22
  88.6 15.0 %collective-permute-start.30 = (f32[3,16,1,128]{3,1,2,0:T(8,128)S(1)}, f32[3,16,1,128]{3,1,2,0:T(8,128)S(1)}, u32[]{:S(2)}, u32[]{:S(2)}) collective-permute-start(f32[3,16,1,128]{3,1,2,0:T(8,128)S(1)} %get-tuple-element.1055), channel_id=1, source_target_pairs={{0,4},{4,8},{8,12},{1,5},{5,9},{9,13},{2,6},{6,10},{10,14},{3,7},{... | collective-permute-start | bytes 73736 | tf_op jit(solution)/shard_map/ppermute | solution.py:21
  92.8 12.2 %collective-permute-start.31 = (f32[3,16,1,128]{3,1,2,0:T(8,128)S(1)}, f32[3,16,1,128]{3,1,2,0:T(8,128)S(1)}, u32[]{:S(2)}, u32[]{:S(2)}) collective-permute-start(f32[3,16,1,128]{3,1,2,0:T(8,128)S(1)} %get-tuple-element.1056), channel_id=1, source_target_pairs={{4,0},{8,4},{12,8},{5,1},{9,5},{13,9},{6,2},{10,6},{14,10},{7,3},{... | collective-permute-start | bytes 73736 | tf_op jit(solution)/shard_map/ppermute | solution.py:22
  94.1 12.3 %collective-permute-start.54 = (f32[3,16,1,128]{3,1,2,0:T(8,128)S(1)}, f32[3,16,1,128]{3,1,2,0:T(8,128)S(1)}, u32[]{:S(2)}, u32[]{:S(2)}) collective-permute-start(f32[3,16,1,128]{3,1,2,0:T(8,128)S(1)} %get-tuple-element.1059), channel_id=1, source_target_pairs={{0,4},{4,8},{8,12},{1,5},{5,9},{9,13},{2,6},{6,10},{10,14},{3,7},{... | collective-permute-start | bytes 73736 | tf_op jit(solution)/shard_map/ppermute | solution.py:21
  98.2 9.5 %collective-permute-start.55 = (f32[3,16,1,128]{3,1,2,0:T(8,128)S(1)}, f32[3,16,1,128]{3,1,2,0:T(8,128)S(1)}, u32[]{:S(2)}, u32[]{:S(2)}) collective-permute-start(f32[3,16,1,128]{3,1,2,0:T(8,128)S(1)} %get-tuple-element.1060), channel_id=1, source_target_pairs={{4,0},{8,4},{12,8},{5,1},{9,5},{13,9},{6,2},{10,6},{14,10},{7,3},{... | collective-permute-start | bytes 73736 | tf_op jit(solution)/shard_map/ppermute | solution.py:22
  99.5 12.3 %collective-permute-start.78 = (f32[3,16,1,128]{3,1,2,0:T(8,128)S(1)}, f32[3,16,1,128]{3,1,2,0:T(8,128)S(1)}, u32[]{:S(2)}, u32[]{:S(2)}) collective-permute-start(f32[3,16,1,128]{3,1,2,0:T(8,128)S(1)} %get-tuple-element.1063), channel_id=1, source_target_pairs={{0,4},{4,8},{8,12},{1,5},{5,9},{9,13},{2,6},{6,10},{10,14},{3,7},{... | collective-permute-start | bytes 73736 | tf_op jit(solution)/shard_map/ppermute | solution.py:21
  103.6 9.5 %collective-permute-start.79 = (f32[3,16,1,128]{3,1,2,0:T(8,128)S(1)}, f32[3,16,1,128]{3,1,2,0:T(8,128)S(1)}, u32[]{:S(2)}, u32[]{:S(2)}) collective-permute-start(f32[3,16,1,128]{3,1,2,0:T(8,128)S(1)} %get-tuple-element.1064), channel_id=1, source_target_pairs={{4,0},{8,4},{12,8},{5,1},{9,5},{13,9},{6,2},{10,6},{14,10},{7,3},{... | collective-permute-start | bytes 73736 | tf_op jit(solution)/shard_map/ppermute | solution.py:22
  104.9 12.3 %collective-permute-start.8 = (f32[3,16,4,1]{3,1,2,0:T(8,128)S(1)}, f32[3,16,4,1]{3,1,2,0:T(8,128)S(1)}, u32[]{:S(2)}, u32[]{:S(2)}) collective-permute-start(f32[3,16,4,1]{3,1,2,0:T(8,128)S(1)} %get-tuple-element.934), channel_id=1, source_target_pairs={{0,2},{1,3},{4,6},{5,7},{8,10},{9,11},{12,14},{13,15},{16,18},{17,... | collective-permute-start | bytes 2312 | tf_op jit(solution)/shard_map/ppermute | solution.py:21
  106.4 12.2 %collective-permute-start.9 = (f32[3,16,4,1]{3,1,2,0:T(8,128)S(1)}, f32[3,16,4,1]{3,1,2,0:T(8,128)S(1)}, u32[]{:S(2)}, u32[]{:S(2)}) collective-permute-start(f32[3,16,4,1]{3,1,2,0:T(8,128)S(1)} %get-tuple-element.935), channel_id=1, source_target_pairs={{2,0},{3,1},{6,4},{7,5},{10,8},{11,9},{14,12},{15,13},{18,16},{19,... | collective-permute-start | bytes 2312 | tf_op jit(solution)/shard_map/ppermute | solution.py:22
  107.7 15.1 %collective-permute-start.32 = (f32[3,16,4,1]{3,1,2,0:T(8,128)S(1)}, f32[3,16,4,1]{3,1,2,0:T(8,128)S(1)}, u32[]{:S(2)}, u32[]{:S(2)}) collective-permute-start(f32[3,16,4,1]{3,1,2,0:T(8,128)S(1)} %get-tuple-element.946), channel_id=1, source_target_pairs={{0,2},{1,3},{4,6},{5,7},{8,10},{9,11},{12,14},{13,15},{16,18},{17,... | collective-permute-start | bytes 2312 | tf_op jit(solution)/shard_map/ppermute | solution.py:21
  111.8 12.3 %collective-permute-start.33 = (f32[3,16,4,1]{3,1,2,0:T(8,128)S(1)}, f32[3,16,4,1]{3,1,2,0:T(8,128)S(1)}, u32[]{:S(2)}, u32[]{:S(2)}) collective-permute-start(f32[3,16,4,1]{3,1,2,0:T(8,128)S(1)} %get-tuple-element.947), channel_id=1, source_target_pairs={{2,0},{3,1},{6,4},{7,5},{10,8},{11,9},{14,12},{15,13},{18,16},{19,... | collective-permute-start | bytes 2312 | tf_op jit(solution)/shard_map/ppermute | solution.py:22
  113.1 11.2 %collective-permute-start.56 = (f32[3,16,4,1]{3,1,2,0:T(8,128)S(1)}, f32[3,16,4,1]{3,1,2,0:T(8,128)S(1)}, u32[]{:S(2)}, u32[]{:S(2)}) collective-permute-start(f32[3,16,4,1]{3,1,2,0:T(8,128)S(1)} %get-tuple-element.950), channel_id=1, source_target_pairs={{0,2},{1,3},{4,6},{5,7},{8,10},{9,11},{12,14},{13,15},{16,18},{17,... | collective-permute-start | bytes 2312 | tf_op jit(solution)/shard_map/ppermute | solution.py:21
  129.1 18.3 %collective-permute-start.10 = (f32[3,1,4,130]{3,1,2,0:T(1,128)S(1)}, f32[3,1,4,130]{3,1,2,0:T(1,128)S(1)}, u32[]{:S(2)}, u32[]{:S(2)}) collective-permute-start(f32[3,1,4,130]{3,1,2,0:T(1,128)S(1)} %get-tuple-element.798), channel_id=1, source_target_pairs={{1,0},{3,2},{5,4},{7,6},{9,8},{11,10},{13,12},{15,14},{17,16},{19,... | collective-permute-start | bytes 18728 | tf_op jit(solution)/shard_map/ppermute | solution.py:22
  136.8 12.0 %collective-permute-start.11 = (f32[3,1,4,130]{3,1,2,0:T(1,128)S(1)}, f32[3,1,4,130]{3,1,2,0:T(1,128)S(1)}, u32[]{:S(2)}, u32[]{:S(2)}) collective-permute-start(f32[3,1,4,130]{3,1,2,0:T(1,128)S(1)} %get-tuple-element.799), channel_id=1, source_target_pairs={{0,1},{2,3},{4,5},{6,7},{8,9},{10,11},{12,13},{14,15},{16,17},{18,... | collective-permute-start | bytes 18728 | tf_op jit(solution)/shard_map/ppermute | solution.py:21
  138.4 13.3 %collective-permute-start.34 = (f32[3,1,4,130]{3,1,2,0:T(1,128)S(1)}, f32[3,1,4,130]{3,1,2,0:T(1,128)S(1)}, u32[]{:S(2)}, u32[]{:S(2)}) collective-permute-start(f32[3,1,4,130]{3,1,2,0:T(1,128)S(1)} %get-tuple-element.802), channel_id=1, source_target_pairs={{1,0},{3,2},{5,4},{7,6},{9,8},{11,10},{13,12},{15,14},{17,16},{19,... | collective-permute-start | bytes 18728 | tf_op jit(solution)/shard_map/ppermute | solution.py:22
  141.5 11.7 %collective-permute-start.35 = (f32[3,1,4,130]{3,1,2,0:T(1,128)S(1)}, f32[3,1,4,130]{3,1,2,0:T(1,128)S(1)}, u32[]{:S(2)}, u32[]{:S(2)}) collective-permute-start(f32[3,1,4,130]{3,1,2,0:T(1,128)S(1)} %get-tuple-element.803), channel_id=1, source_target_pairs={{0,1},{2,3},{4,5},{6,7},{8,9},{10,11},{12,13},{14,15},{16,17},{18,... | collective-permute-start | bytes 18728 | tf_op jit(solution)/shard_map/ppermute | solution.py:21
  143.1 10.1 %collective-permute-start.58 = (f32[3,1,4,130]{3,1,2,0:T(1,128)S(1)}, f32[3,1,4,130]{3,1,2,0:T(1,128)S(1)}, u32[]{:S(2)}, u32[]{:S(2)}) collective-permute-start(f32[3,1,4,130]{3,1,2,0:T(1,128)S(1)} %get-tuple-element.806), channel_id=1, source_target_pairs={{1,0},{3,2},{5,4},{7,6},{9,8},{11,10},{13,12},{15,14},{17,16},{19,... | collective-permute-start | bytes 18728 | tf_op jit(solution)/shard_map/ppermute | solution.py:22
  156.6 10.5 %collective-permute-start.16 = (f32[3,16,2]{1,2,0:T(2,128)S(1)}, f32[3,16,2]{1,2,0:T(2,128)S(1)}, u32[]{:S(2)}, u32[]{:S(2)}) collective-permute-start(f32[3,16,2]{1,2,0:T(2,128)S(1)} %get-tuple-element.663), channel_id=1, source_target_pairs={{2,0},{3,1},{6,4},{7,5},{10,8},{11,9},{14,12},{15,13},{18,16},{19,... | collective-permute-start | bytes 1160 | tf_op jit(solution)/shard_map/ppermute | solution.py:30
  157.9 14.6 %collective-permute-start.14 = (f32[3,16,128]{2,1,0:T(8,128)S(1)}, f32[3,16,128]{2,1,0:T(8,128)S(1)}, u32[]{:S(2)}, u32[]{:S(2)}) collective-permute-start(f32[3,16,128]{2,1,0:T(8,128)S(1)} %get-tuple-element.795), channel_id=1, source_target_pairs={{4,0},{8,4},{12,8},{5,1},{9,5},{13,9},{6,2},{10,6},{14,10},{7,3},{... | collective-permute-start | bytes 73736 | tf_op jit(solution)/shard_map/ppermute | solution.py:30
  159.2 13.1 %collective-permute-start.12 = (f32[3,2,128]{2,1,0:T(2,128)S(1)}, f32[3,2,128]{2,1,0:T(2,128)S(1)}, u32[]{:S(2)}, u32[]{:S(2)}) collective-permute-start(f32[3,2,128]{2,1,0:T(2,128)S(1)} %bitcast.1244), channel_id=1, source_target_pairs={{1,0},{3,2},{5,4},{7,6},{9,8},{11,10},{13,12},{15,14},{17,16},{19,... | collective-permute-start | bytes 9224 | tf_op jit(solution)/shard_map/ppermute | solution.py:30
  161.3 10.9 %collective-permute-start.17 = (f32[3,16,2]{1,2,0:T(2,128)S(1)}, f32[3,16,2]{1,2,0:T(2,128)S(1)}, u32[]{:S(2)}, u32[]{:S(2)}) collective-permute-start(f32[3,16,2]{1,2,0:T(2,128)S(1)} %get-tuple-element.662), channel_id=1, source_target_pairs={{0,2},{1,3},{4,6},{5,7},{8,10},{9,11},{12,14},{13,15},{16,18},{17,... | collective-permute-start | bytes 1160 | tf_op jit(solution)/shard_map/ppermute | solution.py:30
  175.0 16.9 %collective-permute-start.18 = (f32[3,2,128]{2,1,0:T(2,128)S(1)}, f32[3,2,128]{2,1,0:T(2,128)S(1)}, u32[]{:S(2)}, u32[]{:S(2)}) collective-permute-start(f32[3,2,128]{2,1,0:T(2,128)S(1)} %bitcast.1241), channel_id=1, source_target_pairs={{1,0},{3,2},{5,4},{7,6},{9,8},{11,10},{13,12},{15,14},{17,16},{19,... | collective-permute-start | bytes 9224 | tf_op jit(solution)/shard_map/ppermute | solution.py:30
  180.4 11.6 %collective-permute-start.20 = (f32[3,16,128]{2,1,0:T(8,128)S(1)}, f32[3,16,128]{2,1,0:T(8,128)S(1)}, u32[]{:S(2)}, u32[]{:S(2)}) collective-permute-start(f32[3,16,128]{2,1,0:T(8,128)S(1)} %get-tuple-element.790), channel_id=1, source_target_pairs={{4,0},{8,4},{12,8},{5,1},{9,5},{13,9},{6,2},{10,6},{14,10},{7,3},{... | collective-permute-start | bytes 73736 | tf_op jit(solution)/shard_map/ppermute | solution.py:30
  181.8 10.0 %collective-permute-start.23 = (f32[3,16,2]{1,2,0:T(2,128)S(1)}, f32[3,16,2]{1,2,0:T(2,128)S(1)}, u32[]{:S(2)}, u32[]{:S(2)}) collective-permute-start(f32[3,16,2]{1,2,0:T(2,128)S(1)} %get-tuple-element.660), channel_id=1, source_target_pairs={{0,2},{1,3},{4,6},{5,7},{8,10},{9,11},{12,14},{13,15},{16,18},{17,... | collective-permute-start | bytes 1160 | tf_op jit(solution)/shard_map/ppermute | solution.py:30
  194.5 17.0 %collective-permute-start.36 = (f32[3,2,128]{2,1,0:T(2,128)S(1)}, f32[3,2,128]{2,1,0:T(2,128)S(1)}, u32[]{:S(2)}, u32[]{:S(2)}) collective-permute-start(f32[3,2,128]{2,1,0:T(2,128)S(1)} %bitcast.1268), channel_id=1, source_target_pairs={{1,0},{3,2},{5,4},{7,6},{9,8},{11,10},{13,12},{15,14},{17,16},{19,... | collective-permute-start | bytes 9224 | tf_op jit(solution)/shard_map/ppermute | solution.py:30
  199.9 11.6 %collective-permute-start.37 = (f32[3,2,128]{2,1,0:T(2,128)S(1)}, f32[3,2,128]{2,1,0:T(2,128)S(1)}, u32[]{:S(2)}, u32[]{:S(2)}) collective-permute-start(f32[3,2,128]{2,1,0:T(2,128)S(1)} %bitcast.1271), channel_id=1, source_target_pairs={{0,1},{2,3},{4,5},{6,7},{8,9},{10,11},{12,13},{14,15},{16,17},{18,... | collective-permute-start | bytes 9224 | tf_op jit(solution)/shard_map/ppermute | solution.py:30
  201.3 10.0 %collective-permute-start.41 = (f32[3,16,2]{1,2,0:T(2,128)S(1)}, f32[3,16,2]{1,2,0:T(2,128)S(1)}, u32[]{:S(2)}, u32[]{:S(2)}) collective-permute-start(f32[3,16,2]{1,2,0:T(2,128)S(1)} %bitcast.1257), channel_id=1, source_target_pairs={{0,2},{1,3},{4,6},{5,7},{8,10},{9,11},{12,14},{13,15},{16,18},{17,... | collective-permute-start | bytes 1160 | tf_op jit(solution)/shard_map/ppermute | solution.py:30
  214.0 17.1 %collective-permute-start.42 = (f32[3,2,128]{2,1,0:T(2,128)S(1)}, f32[3,2,128]{2,1,0:T(2,128)S(1)}, u32[]{:S(2)}, u32[]{:S(2)}) collective-permute-start(f32[3,2,128]{2,1,0:T(2,128)S(1)} %bitcast.1242), channel_id=1, source_target_pairs={{1,0},{3,2},{5,4},{7,6},{9,8},{11,10},{13,12},{15,14},{17,16},{19,... | collective-permute-start | bytes 9224 | tf_op jit(solution)/shard_map/ppermute | solution.py:30
  219.7 11.6 %collective-permute-start.44 = (f32[3,16,128]{2,1,0:T(8,128)S(1)}, f32[3,16,128]{2,1,0:T(8,128)S(1)}, u32[]{:S(2)}, u32[]{:S(2)}) collective-permute-start(f32[3,16,128]{2,1,0:T(8,128)S(1)} %get-tuple-element.779), channel_id=1, source_target_pairs={{4,0},{8,4},{12,8},{5,1},{9,5},{13,9},{6,2},{10,6},{14,10},{7,3},{... | collective-permute-start | bytes 73736 | tf_op jit(solution)/shard_map/ppermute | solution.py:30
  221.1 10.0 %collective-permute-start.47 = (f32[3,16,2]{1,2,0:T(2,128)S(1)}, f32[3,16,2]{1,2,0:T(2,128)S(1)}, u32[]{:S(2)}, u32[]{:S(2)}) collective-permute-start(f32[3,16,2]{1,2,0:T(2,128)S(1)} %get-tuple-element.658), channel_id=1, source_target_pairs={{0,2},{1,3},{4,6},{5,7},{8,10},{9,11},{12,14},{13,15},{16,18},{17,... | collective-permute-start | bytes 1160 | tf_op jit(solution)/shard_map/ppermute | solution.py:30
  233.8 17.0 %collective-permute-start.60 = (f32[3,2,128]{2,1,0:T(2,128)S(1)}, f32[3,2,128]{2,1,0:T(2,128)S(1)}, u32[]{:S(2)}, u32[]{:S(2)}) collective-permute-start(f32[3,2,128]{2,1,0:T(2,128)S(1)} %bitcast.1269), channel_id=1, source_target_pairs={{1,0},{3,2},{5,4},{7,6},{9,8},{11,10},{13,12},{15,14},{17,16},{19,... | collective-permute-start | bytes 9224 | tf_op jit(solution)/shard_map/ppermute | solution.py:30
  239.2 11.6 %collective-permute-start.61 = (f32[3,2,128]{2,1,0:T(2,128)S(1)}, f32[3,2,128]{2,1,0:T(2,128)S(1)}, u32[]{:S(2)}, u32[]{:S(2)}) collective-permute-start(f32[3,2,128]{2,1,0:T(2,128)S(1)} %bitcast.1272), channel_id=1, source_target_pairs={{0,1},{2,3},{4,5},{6,7},{8,9},{10,11},{12,13},{14,15},{16,17},{18,... | collective-permute-start | bytes 9224 | tf_op jit(solution)/shard_map/ppermute | solution.py:30
  240.6 10.0 %collective-permute-start.65 = (f32[3,16,2]{1,2,0:T(2,128)S(1)}, f32[3,16,2]{1,2,0:T(2,128)S(1)}, u32[]{:S(2)}, u32[]{:S(2)}) collective-permute-start(f32[3,16,2]{1,2,0:T(2,128)S(1)} %bitcast.1261), channel_id=1, source_target_pairs={{0,2},{1,3},{4,6},{5,7},{8,10},{9,11},{12,14},{13,15},{16,18},{17,... | collective-permute-start | bytes 1160 | tf_op jit(solution)/shard_map/ppermute | solution.py:30
  253.3 17.1 %collective-permute-start.66 = (f32[3,2,128]{2,1,0:T(2,128)S(1)}, f32[3,2,128]{2,1,0:T(2,128)S(1)}, u32[]{:S(2)}, u32[]{:S(2)}) collective-permute-start(f32[3,2,128]{2,1,0:T(2,128)S(1)} %bitcast.1243), channel_id=1, source_target_pairs={{1,0},{3,2},{5,4},{7,6},{9,8},{11,10},{13,12},{15,14},{17,16},{19,... | collective-permute-start | bytes 9224 | tf_op jit(solution)/shard_map/ppermute | solution.py:30
  258.9 11.6 %collective-permute-start.68 = (f32[3,16,128]{2,1,0:T(8,128)S(1)}, f32[3,16,128]{2,1,0:T(8,128)S(1)}, u32[]{:S(2)}, u32[]{:S(2)}) collective-permute-start(f32[3,16,128]{2,1,0:T(8,128)S(1)} %get-tuple-element.768), channel_id=1, source_target_pairs={{4,0},{8,4},{12,8},{5,1},{9,5},{13,9},{6,2},{10,6},{14,10},{7,3},{... | collective-permute-start | bytes 73736 | tf_op jit(solution)/shard_map/ppermute | solution.py:30
  260.3 10.0 %collective-permute-start.71 = (f32[3,16,2]{1,2,0:T(2,128)S(1)}, f32[3,16,2]{1,2,0:T(2,128)S(1)}, u32[]{:S(2)}, u32[]{:S(2)}) collective-permute-start(f32[3,16,2]{1,2,0:T(2,128)S(1)} %get-tuple-element.656), channel_id=1, source_target_pairs={{0,2},{1,3},{4,6},{5,7},{8,10},{9,11},{12,14},{13,15},{16,18},{17,... | collective-permute-start | bytes 1160 | tf_op jit(solution)/shard_map/ppermute | solution.py:30
  273.0 17.0 %collective-permute-start.84 = (f32[3,2,128]{2,1,0:T(2,128)S(1)}, f32[3,2,128]{2,1,0:T(2,128)S(1)}, u32[]{:S(2)}, u32[]{:S(2)}) collective-permute-start(f32[3,2,128]{2,1,0:T(2,128)S(1)} %bitcast.1270), channel_id=1, source_target_pairs={{1,0},{3,2},{5,4},{7,6},{9,8},{11,10},{13,12},{15,14},{17,16},{19,... | collective-permute-start | bytes 9224 | tf_op jit(solution)/shard_map/ppermute | solution.py:30
  278.5 11.6 %collective-permute-start.85 = (f32[3,2,128]{2,1,0:T(2,128)S(1)}, f32[3,2,128]{2,1,0:T(2,128)S(1)}, u32[]{:S(2)}, u32[]{:S(2)}) collective-permute-start(f32[3,2,128]{2,1,0:T(2,128)S(1)} %bitcast.1273), channel_id=1, source_target_pairs={{0,1},{2,3},{4,5},{6,7},{8,9},{10,11},{12,13},{14,15},{16,17},{18,... | collective-permute-start | bytes 9224 | tf_op jit(solution)/shard_map/ppermute | solution.py:30
  279.9 10.0 %collective-permute-start.89 = (f32[3,16,2]{1,2,0:T(2,128)S(1)}, f32[3,16,2]{1,2,0:T(2,128)S(1)}, u32[]{:S(2)}, u32[]{:S(2)}) collective-permute-start(f32[3,16,2]{1,2,0:T(2,128)S(1)} %bitcast.1265), channel_id=1, source_target_pairs={{0,2},{1,3},{4,6},{5,7},{8,10},{9,11},{12,14},{13,15},{16,18},{17,... | collective-permute-start | bytes 1160 | tf_op jit(solution)/shard_map/ppermute | solution.py:30
  310.7 20.6 %collective-permute-start.90 = (f32[3,2,128]{2,1,0:T(2,128)S(1)}, f32[3,2,128]{2,1,0:T(2,128)S(1)}, u32[]{:S(2)}, u32[]{:S(2)}) collective-permute-start(f32[3,2,128]{2,1,0:T(2,128)S(1)} %bitcast.1236), channel_id=1, source_target_pairs={{1,0},{3,2},{5,4},{7,6},{9,8},{11,10},{13,12},{15,14},{17,16},{19,... | collective-permute-start | bytes 9224 | tf_op jit(solution)/shard_map/ppermute | solution.py:30
  320.4 11.1 %collective-permute-start.92 = (f32[3,16,128]{2,1,0:T(8,128)S(1)}, f32[3,16,128]{2,1,0:T(8,128)S(1)}, u32[]{:S(2)}, u32[]{:S(2)}) collective-permute-start(f32[3,16,128]{2,1,0:T(8,128)S(1)} %get-tuple-element.757), channel_id=1, source_target_pairs={{4,0},{8,4},{12,8},{5,1},{9,5},{13,9},{6,2},{10,6},{14,10},{7,3},{... | collective-permute-start | bytes 73736 | tf_op jit(solution)/shard_map/ppermute | solution.py:30
  321.8 9.4 %collective-permute-start.95 = (f32[3,16,2]{1,2,0:T(2,128)S(1)}, f32[3,16,2]{1,2,0:T(2,128)S(1)}, u32[]{:S(2)}, u32[]{:S(2)}) collective-permute-start(f32[3,16,2]{1,2,0:T(2,128)S(1)} %get-tuple-element.654), channel_id=1, source_target_pairs={{0,2},{1,3},{4,6},{5,7},{8,10},{9,11},{12,14},{13,15},{16,18},{17,... | collective-permute-start | bytes 1160 | tf_op jit(solution)/shard_map/ppermute | solution.py:30
  (37 other events, 214.3 us)
where the time goes:
time: 338 us; the launch traced here: 333 us
  starting transfers between devices  260 us (77%)
  local copies, waits for them, and re-layouts  18.6 us (6%)
  other arithmetic  17.4 us (5%)
  blocking collectives  17.1 us (5%)
  waiting for transfers between devices  16.3 us (5%)
  between operations  3.76 us (1%)
    ppermute x48, starting transfers between devices, passed_along(): return lax.ppermute(block, axis, route)  133 us
    ppermute x24, starting transfers between devices, with_halo(): before = lax.ppermute(last, axis, up)  69.2 us
    ppermute x24, starting transfers between devices, with_halo(): after = lax.ppermute(initial, axis, down)  54 us
    psum x1, blocking collectives, on_device(): summed_drag, summed_cost = lax.psum((seg_drag, seg_cost), ('gx', 'col'))  17.1 us
    ppermute x24, waiting for transfers between devices, with_halo(): after = lax.ppermute(initial, axis, down)  8.39 us
    unnamed x16, local copies, waits for them, and re-layouts  7.13 us
  transfers between devices with their start and end apart: 97, of which 13 were waited for; matrix products, arithmetic and copies ran while one was open for 3% of the time, Pallas kernels for 0%

commit v1 on v0

--- a/solution.py
+++ b/solution.py
@@ -1,6 +1,10 @@
+import functools
+
 import jax
 import jax.numpy as jnp
 from jax import lax
+from jax.experimental import pallas as pl
+from jax.experimental.pallas import tpu as pltpu
 from jax.sharding import PartitionSpec as P
 
 SEG = 2
@@ -150,9 +154,408 @@
     return (adjoint, cost * scale, drag_total * scale)
 
 
+MESH = pl.DeviceIdType.MESH
+UNSEEN = 1e30
+TILE = 8
+PAD = 8
+
+
+def sweep_kernel(
+    zn, levels, lat, lon, ck, obs, mask, drag, out, cost, dgrad,
+    ckg, omg, dragb, xs, lam, acc, send, rck, rom, rdrag,
+):
+    local_segs = ck.shape[0]
+    segments = obs.shape[0]
+    x, c, g = (lax.axis_index(a) for a in ("gx", "col", "gz"))
+    oc, og = 1 - c, 1 - g
+    half = levels * lat
+    total = 2 * half
+    wide = 2 * lon
+    mine = pl.ds(pl.multiple_of(g * half, half), half)
+    theirs = pl.ds(pl.multiple_of(og * half, half), half)
+    started = []
+
+    def put(src, dst, sem, where):
+        copy = pltpu.make_async_remote_copy(
+            src_ref=src, dst_ref=dst, send_sem=send.at[len(started)], recv_sem=sem,
+            device_id=where, device_id_type=MESH,
+        )
+        copy.start()
+        started.append(copy)
+
+    def arrived(dst, sem):
+        pltpu.make_async_remote_copy(
+            src_ref=dst, dst_ref=dst, send_sem=send.at[0], recv_sem=sem,
+            device_id={"gz": og}, device_id_type=MESH,
+        ).wait_recv()
+
+    z_peers = [lax.rem(x + d, zn) for d in range(1, zn)]
+    z_from = [lax.rem(x + zn - d, zn) for d in range(1, zn)]
+
+    barrier = pltpu.get_barrier_semaphore()
+    for p in z_peers:
+        pl.semaphore_signal(barrier, inc=1, device_id={"gx": p}, device_id_type=MESH)
+    pl.semaphore_signal(barrier, inc=1, device_id={"col": oc}, device_id_type=MESH)
+    pl.semaphore_signal(barrier, inc=1, device_id={"gz": og}, device_id_type=MESH)
+
+    for s in range(segments):
+        omg[s, c, x, mine, :] = jnp.where(mask[s] != 0, obs[s], UNSEEN)
+    lane = lax.broadcasted_iota(jnp.int32, (half, levels), 1)
+    sub = lax.broadcasted_iota(jnp.int32, (half, levels), 0)
+    spread = jnp.sum(
+        jnp.where(sub // lat == lane, jnp.broadcast_to(drag[...], (half, levels)), 0.0),
+        axis=1, keepdims=True,
+    )
+    dragb[mine, :] = jnp.broadcast_to(spread, (half, lon))
+    pl.semaphore_wait(barrier, zn + 1)
+
+    halves = [pl.ds(segments // 2, segments - segments // 2), pl.ds(0, segments // 2)]
+
+    def ck_at(s, z, rows):
+        return ckg.at[s, :, z, rows, :]
+
+    def om_at(b, col, z, rows):
+        return omg.at[halves[b], col, z, rows, :]
+
+    rim_n = half // 2
+    rim = pl.ds(pl.multiple_of(og * (half - rim_n) + g * half, rim_n), rim_n)
+    other_rim = pl.ds(pl.multiple_of(g * (half - rim_n) + og * half, rim_n), rim_n)
+
+    order = list(reversed(range(local_segs)))
+    own = [c * local_segs + j for j in range(local_segs)]
+    far = [oc * local_segs + j for j in range(local_segs)]
+
+    for j in order:
+        for p in z_peers:
+            put(ck.at[j], ck_at(own[j], x, mine), rck.at[own[j], x, g], {"gx": p})
+        put(ck.at[j], ck_at(own[j], x, mine), rck.at[own[j], x, g], {"col": oc})
+    for b in range(2):
+        put(om_at(b, c, x, mine), om_at(b, c, x, mine), rom.at[b, c, x, g], {"col": oc})
+        for p in z_peers:
+            put(om_at(b, c, x, mine), om_at(b, c, x, mine), rom.at[b, c, x, g], {"gx": p})
+    put(dragb.at[mine], dragb.at[mine], rdrag, {"gz": og})
+    for j in order:
+        put(ck.at[j], ck_at(own[j], x, mine), rck.at[own[j], x, g], {"gz": og})
+    for b in range(2):
+        put(om_at(b, c, x, rim), om_at(b, c, x, rim), rom.at[b, c, x, g], {"gz": og})
+    for j in order:
+        ckg[own[j], :, x, mine, :] = ck[j]
+
+    xs[...] = jnp.zeros_like(xs)
+    lam[...] = jnp.zeros_like(lam)
+    acc[...] = jnp.zeros_like(acc)
+
+    for j in order:
+        for z in z_from:
+            here, sem = ck_at(own[j], z, mine), rck.at[own[j], z, g]
+            arrived(here, sem)
+            put(here, here, sem, {"col": oc})
+            put(here, here, sem, {"gz": og})
+    for b in range(2):
+        here, sem = om_at(b, oc, x, mine), rom.at[b, oc, x, g]
+        arrived(here, sem)
+        for p in z_peers:
+            put(here, here, sem, {"gx": p})
+        edge = om_at(b, oc, x, rim)
+        put(edge, edge, sem, {"gz": og})
+    for b in range(2):
+        for z in z_from:
+            arrived(om_at(b, c, z, mine), rom.at[b, c, z, g])
+            edge = om_at(b, c, z, rim)
+            put(edge, edge, rom.at[b, c, z, g], {"gz": og})
+    for j in order:
+        for z in range(zn):
+            here, sem = ck_at(far[j], z, mine), rck.at[far[j], z, g]
+            arrived(here, sem)
+            put(here, here, sem, {"gz": og})
+    for b in range(2):
+        for z in z_from:
+            arrived(om_at(b, oc, z, mine), rom.at[b, oc, z, g])
+            edge = om_at(b, oc, z, rim)
+            put(edge, edge, rom.at[b, oc, z, g], {"gz": og})
+    arrived(dragb.at[theirs], rdrag)
+
+    at_lane = lax.broadcasted_iota(jnp.int32, (TILE, wide), 1)
+    at_row = lax.broadcasted_iota(jnp.int32, (TILE, wide), 0) % lat
+    first_lane, last_lane = at_lane == 0, at_lane == wide - 1
+    first_row, last_row = at_row == 0, at_row == lat - 1
+    row_f = at_row.astype(jnp.float32)
+    total_lat, total_lon = float(zn * lat), float(wide)
+    col_weight = 1.0 + 2.0 * at_lane.astype(jnp.float32) / total_lon
+    coriolis = [time_step * (0.2 + 0.1 * (row_f + float(z * lat)) / total_lat) for z in range(zn)]
+    weights = [(1.0 + 2.0 * (row_f + float(z * lat)) / total_lat) * col_weight for z in range(zn)]
+    half_step = 0.5 * time_step
+    keep = 1.0 - 4.0 * viscosity - 2.0 * vertical_mix
+
+    def east(a):
+        return jnp.where(last_lane, 0.0, pltpu.roll(a, wide - 1, 1))
+
+    def west(a):
+        return jnp.where(first_lane, 0.0, pltpu.roll(a, 1, 1))
+
+    def at(ref, lead, f, z, o, shift):
+        return jnp.concatenate(
+            [ref[lead, f, z + 1, t, pl.ds(o + shift, TILE), :] for t in range(2)], axis=1
+        )
+
+    def keep_at(ref, lead, f, z, m, value):
+        spot = pl.ds(pl.multiple_of(m + PAD, TILE), TILE)
+        for t in range(2):
+            ref[lead, f, z + 1, t, spot, :] = value[:, t * lon : (t + 1) * lon]
+
+    def north(ref, lead, f, z, o):
+        return jnp.where(
+            last_row, at(ref, lead, f, z + 1, o, 1 - lat), at(ref, lead, f, z, o, 1)
+        )
+
+    def south(ref, lead, f, z, o):
+        return jnp.where(
+            first_row, at(ref, lead, f, z - 1, o, lat - 1), at(ref, lead, f, z, o, -1)
+        )
+
+    def mixed(ref, lead, f, z, o):
+        return at(ref, lead, f, z, o, lat) + at(ref, lead, f, z, o, -lat)
+
+    def rates(m):
+        d = dragb[pl.ds(m, TILE), :] * time_step
+        return jnp.concatenate([d, d], axis=1)
+
+    def step(src, z, o, m, dt_drag):
+        h, u, v = (at(xs, src, f, z, o, 0) for f in range(3))
+        h_e, u_e, v_e = east(h), east(u), east(v)
+        h_w, u_w, v_w = west(h), west(u), west(v)
+        h_n, u_n, v_n = (north(xs, src, f, z, o) for f in range(3))
+        h_s, u_s, v_s = (south(xs, src, f, z, o) for f in range(3))
+        u_dx, u_dy = u_e - u_w, u_n - u_s
+        v_dx, v_dy = v_e - v_w, v_n - v_s
+        h_new = (
+            keep * h
+            + viscosity * ((h_n + h_s) + (h_e + h_w))
+            - half_step * ((u_dx + v_dy) + (h_e * u_e - h_w * u_w) + (h_n * v_n - h_s * v_s))
+            + vertical_mix * mixed(xs, src, 0, z, o)
+        )
+        u_new = (
+            keep * u
+            + viscosity * ((u_n + u_s) + (u_e + u_w))
+            - half_step * ((h_e - h_w) + u * u_dx + v * u_dy)
+            + (coriolis[z] * v - dt_drag * u)
+            + vertical_mix * mixed(xs, src, 1, z, o)
+        )
+        v_new = (
+            keep * v
+            + viscosity * ((v_n + v_s) + (v_e + v_w))
+            - half_step * ((h_n - h_s) + u * v_dx + v * v_dy)
+            - (coriolis[z] * u + dt_drag * v)
+            + vertical_mix * mixed(xs, src, 2, z, o)
+        )
+        return h_new, u_new, v_new
+
+    def thickness(src, z, o):
+        h, u, v = (at(xs, src, f, z, o, 0) for f in range(3))
+        h_e, u_e, h_w, u_w = east(h), east(u), west(h), west(u)
+        h_n, v_n = (north(xs, src, f, z, o) for f in (0, 2))
+        h_s, v_s = (south(xs, src, f, z, o) for f in (0, 2))
+        return (
+            keep * h
+            + viscosity * ((h_n + h_s) + (h_e + h_w))
+            - half_step
+            * ((u_e - u_w) + (v_n - v_s) + (h_e * u_e - h_w * u_w) + (h_n * v_n - h_s * v_s))
+            + vertical_mix * mixed(xs, src, 0, z, o)
+        )
+
+    def adjoint(src, lead, z, o, dt_drag):
+        h, u, v = (at(xs, src, f, z, o, 0) for f in range(3))
+        a, b, d = (at(lam, lead, f, z, o, 0) for f in range(3))
+        u_e, v_e, u_w, v_w = east(u), east(v), west(u), west(v)
+        u_n, v_n = (north(xs, src, f, z, o) for f in (1, 2))
+        u_s, v_s = (south(xs, src, f, z, o) for f in (1, 2))
+        a_e, b_e, d_e = east(a), east(b), east(d)
+        a_w, b_w, d_w = west(a), west(b), west(d)
+        a_n, b_n, d_n = (north(lam, lead, f, z, o) for f in range(3))
+        a_s, b_s, d_s = (south(lam, lead, f, z, o) for f in range(3))
+        a_dx, a_dy = a_e - a_w, a_n - a_s
+        deep = 1.0 + h
+        new_a = (
+            keep * a
+            + viscosity * ((a_n + a_s) + (a_e + a_w))
+            + half_step * ((b_e - b_w) + (d_n - d_s) + u * a_dx + v * a_dy)
+            + vertical_mix * mixed(lam, lead, 0, z, o)
+        )
+        new_b = (
+            keep * b
+            + viscosity * ((b_n + b_s) + (b_e + b_w))
+            + half_step
+            * (
+                (u_e * b_e - u_w * b_w)
+                + (v_n * b_n - v_s * b_s)
+                + deep * a_dx
+                - (b * (u_e - u_w) + d * (v_e - v_w))
+            )
+            - (dt_drag * b + coriolis[z] * d)
+            + vertical_mix * mixed(lam, lead, 1, z, o)
+        )
+        new_d = (
+            keep * d
+            + viscosity * ((d_n + d_s) + (d_e + d_w))
+            + half_step
+            * (
+                (u_e * d_e - u_w * d_w)
+                + (v_n * d_n - v_s * d_s)
+                + deep * a_dy
+                - (b * (u_n - u_s) + d * (v_n - v_s))
+            )
+            + (coriolis[z] * b - dt_drag * d)
+            + vertical_mix * mixed(lam, lead, 2, z, o)
+        )
+        return (new_a, new_b, new_d), u * b + v * d
+
+    def over(reach, work):
+        count = min(total, half + -(-reach * lat // TILE) * TILE) // TILE
+        begin = g * (total - count * TILE)
+
+        def body(i, carry):
+            m = pl.multiple_of(begin + i * TILE, TILE)
+            work(m)
+            return carry
+
+        lax.fori_loop(0, count, body, 0)
+
+    now = 0
+    for seg in reversed(range(segments)):
+        remaining = SEG * (seg + 1)
+        owner, b = seg // local_segs, 0 if seg >= segments // 2 else 1
+        for z in range(zn):
+            arrived(ck_at(seg, z, theirs), rck.at[seg, z, og])
+        if seg == segments - 1 or seg == segments // 2 - 1:
+            for col in range(2):
+                for z in range(zn):
+                    arrived(om_at(b, col, z, other_rim), rom.at[b, col, z, og])
+        for f in range(3):
+            for z in range(zn):
+                for t in range(2):
+                    part = ckg[seg, f, z, :, t * lon : (t + 1) * lon]
+                    xs[0, f, z + 1, t, pl.ds(PAD, total), :] = part.astype(jnp.float32)
+
+        def first(m):
+            dt_drag = rates(m)
+            for z in range(zn):
+                for f, value in enumerate(step(0, z, m + PAD, m, dt_drag)):
+                    keep_at(xs, 1, f, z, m, value)
+
+        over(remaining + 1, first)
+
+        def force(m):
+            spent = jnp.zeros((TILE, wide), jnp.float32)
+            for z in range(zn):
+                seen = jnp.concatenate(
+                    [omg[seg, col, z, pl.ds(m, TILE), :] for col in range(2)], axis=1
+                )
+                resid = jnp.where(seen < 0.5 * UNSEEN, thickness(1, z, m + PAD) - seen, 0.0)
+                forcing = weights[z] * resid
+                spent = spent + forcing * resid
+                keep_at(lam, now, 0, z, m, at(lam, now, 0, z, pl.multiple_of(m + PAD, TILE), 0) + forcing)
+            acc[0, pl.ds(m, TILE), :] = acc[0, pl.ds(m, TILE), :] + spent
+
+        over(remaining, force)
+        for n in reversed(range(SEG)):
+            remaining -= 1
+            later = 1 - now
+
+            def back(m):
+                dt_drag = rates(m)
+                pull = jnp.zeros((TILE, wide), jnp.float32)
+                for z in range(zn):
+                    new, part = adjoint(n, now, z, m + PAD, dt_drag)
+                    pull = pull + part
+                    for f, value in enumerate(new):
+                        keep_at(lam, later, f, z, m, value)
+                acc[1, pl.ds(m, TILE), :] = acc[1, pl.ds(m, TILE), :] + pull
+
+            over(remaining, back)
+            now = later
+
+    spot = pl.ds(pl.multiple_of(g * half + PAD, TILE), half)
+    for f in range(3):
+        out[f] = lam[now, f, x + 1, c, spot, :]
+    scale = 1.0 / (total_lat * total_lon)
+    level = lax.broadcasted_iota(jnp.int32, (half, lon), 0) // lat
+    pick = level == lax.broadcasted_iota(jnp.int32, (half, lon), 1)
+    for k, (ref, factor) in enumerate(((cost, 0.5 * scale), (dgrad, -time_step * scale))):
+        sums = jnp.sum(acc[k, mine, :], axis=1, keepdims=True)
+        line = jnp.sum(jnp.where(pick, sums, 0.0), axis=0, keepdims=True)
+        ref[...] = factor * line[:, :levels]
+    for copy in started:
+        copy.wait_send()
+
+
+def gathered(zn, checkpoints, obs_values, obs_mask, drag):
+    segments, levels, lat, lon = obs_values.shape
+    half, wide = levels * lat, 2 * lon
+    local_segs = checkpoints.shape[0]
+    sends = local_segs * ((zn + 1) + 2 * (zn - 1) + zn) + 2 * (zn + 1 + zn + 2 * (zn - 1)) + 1
+    f32 = jnp.float32
+    out, cost, pull = pl.pallas_call(
+        functools.partial(sweep_kernel, zn, levels, lat, lon),
+        out_shape=(
+            jax.ShapeDtypeStruct((3, half, lon), f32),
+            jax.ShapeDtypeStruct((1, levels), f32),
+            jax.ShapeDtypeStruct((1, levels), f32),
+        ),
+        in_specs=[pl.BlockSpec(memory_space=pltpu.VMEM)] * 4,
+        out_specs=[pl.BlockSpec(memory_space=pltpu.VMEM)] * 3,
+        scratch_shapes=[
+            pltpu.VMEM((segments, 3, zn, 2 * half, wide), checkpoints.dtype),
+            pltpu.VMEM((segments, 2, zn, 2 * half, lon), f32),
+            pltpu.VMEM((2 * half, lon), f32),
+            pltpu.VMEM((2, 3, zn + 2, 2, 2 * half + 2 * PAD, lon), f32),
+            pltpu.VMEM((2, 3, zn + 2, 2, 2 * half + 2 * PAD, lon), f32),
+            pltpu.VMEM((2, 2 * half, wide), f32),
+            pltpu.SemaphoreType.DMA((sends + 8,)),
+            pltpu.SemaphoreType.DMA((segments, zn, 2)),
+            pltpu.SemaphoreType.DMA((2, 2, zn, 2)),
+            pltpu.SemaphoreType.DMA,
+        ],
+        compiler_params=pltpu.CompilerParams(
+            collective_id=0, has_side_effects=True, vmem_limit_bytes=48 * 2**20
+        ),
+        name="sweep",
+    )(
+        checkpoints.reshape(local_segs, 3, half, wide),
+        obs_values.reshape(segments, half, lon),
+        obs_mask.reshape(segments, half, lon),
+        drag.reshape(1, levels),
+    )
+    return out.reshape(3, levels, lat, lon), cost.reshape(levels), pull.reshape(levels)
+
+
+def choose(sizes, checkpoints, obs_values, obs_mask, drag):
+    segments, levels, lat, lon = obs_values.shape
+    zn = sizes["gx"]
+    half = levels * lat
+    cells = zn * 2 * half * 2 * lon
+    room = cells * (segments * (3 * 2 + 4) + 15 * 4)
+    fits = (
+        sizes["col"] == 2
+        and sizes["gz"] == 2
+        and room < 32 * 2**20
+        and zn > 1
+        and lat <= PAD
+        and half % (4 * TILE) == 0
+        and lon == 128
+        and segments % 2 == 0
+        and levels >= 2 * (SEG * segments + 1) - levels
+        and half // 2 >= SEG * segments * lat
+        and levels <= lon
+    )
+    if fits:
+        return gathered(zn, checkpoints, obs_values, obs_mask, drag)
+    return on_device(checkpoints, obs_values, obs_mask, drag)
+
+
 def solution(mesh):
+    sizes = dict(mesh.shape)
     return jax.shard_map(
-        on_device,
+        functools.partial(choose, sizes),
         mesh=mesh,
         in_specs=(
             P(("ens", "col"), None, "gz", "gx", None),

time: 338 us -> 44.3 us (0.13); the launches traced: 333 us -> 44.1 us
  starting transfers between devices: 260 us -> 0 us
  Pallas kernels: 0 us -> 40.7 us
  other arithmetic: 17.4 us -> 0 us
  blocking collectives: 17.1 us -> 0 us
  waiting for transfers between devices: 16.3 us -> 0 us
  local copies, waits for them, and re-layouts: 18.6 us -> 2.64 us
    ppermute x96 -> x0, starting transfers between devices: 257 us -> none  [the longest x48 133 us: passed_along(): return lax.ppermute(block, axis, route)]
    pallas_call x0 -> x1, Pallas kernels: none -> 40.7 us  [gathered(): pl.pallas_call(functools.partial(sweep_kernel, zn, levels, lat, lon), out...]
    psum x1 -> x0, blocking collectives: 17.1 us -> none  [on_device(): summed_drag, summed_cost = lax.psum((seg_drag, seg_cost), ('gx', 'col'))]
    ppermute x96 -> x0, waiting for transfers between devices: 14.4 us -> none  [the longest x24 8.39 us: with_halo(): after = lax.ppermute(initial, axis, down)]
    scatter-add x35 -> x0, local copies, waits for them, and re-layouts: 5.73 us -> none  [the longest x16 5.01 us: halo_back(): return inner.at[:, :, :, -1].add(west).at[:, :, :, 0].add(east)]
    unnamed x16 -> x9, local copies, waits for them, and re-layouts: 7.13 us -> 1.66 us
    broadcast_in_dim x32 -> x0, other arithmetic: 4.23 us -> none  [the longest x24 3.4 us: advance(): thick, zonal, merid = (levels[0], levels[1], levels[2])]
    all_to_all x1 -> x0, starting transfers between devices: 3.47 us -> none  [on_device(): lax.all_to_all(checkpoints, 'col', split_axis=4, concat_axis=0, tiled=True)]
  transfers between devices with their start and end apart: 97 -> 0, of which waited for: 13 -> 0; matrix products, arithmetic and copies ran while one was open for 3% -> 0% of each run, Pallas kernels for 0% -> 0%
where the time goes in v1:
time: 44.3 us; the launch traced here: 44.1 us
  Pallas kernels  40.7 us (92%)
  local copies, waits for them, and re-layouts  2.64 us (6%)
  between operations  0.69 us (2%)
    pallas_call x1, Pallas kernels, gathered(): pl.pallas_call(functools.partial(sweep_kernel, zn, levels, lat, lon), out...  40.7 us
    unnamed x9, local copies, waits for them, and re-layouts  1.66 us
    reshape x1, local copies, waits for them, and re-layouts, gathered(): checkpoints.reshape(local_segs, 3, half, wide)  0.98 us

profile of v1, /device:TPU:1, one launch (start us, length us, event | category | flops | bytes accessed | tf_op | source)
XLA Modules:
  0.0 44.1 jit_solution(701538059514591742)
XLA Ops:
  0.6 0.0 copy-start
  0.6 0.0 copy-start.1
  0.7 0.0 copy-start.2
  0.7 1.0 %reshape.27.ck = bf16[2,3,32,256]{3,2,1,0:T(8,128)(2,1)S(1)} reshape(bf16[2,3,16,2,256]{4,3,2,1,0:T(2,128)(2,1)} %param.4) | data formatting | bytes 196608 | tf_op jit(solution)/shard_map/reshape | solution.py:523
  1.6 0.0 copy-done
  1.7 0.0 copy-done.1
  1.7 0.0 copy-done.2
  1.7 40.7 %sweep.1 = (f32[3,32,128]{2,1,0:T(8,128)S(1)}, f32[1,16]{1,0:T(1,128)S(1)}, f32[1,16]{1,0:T(1,128)S(1)}) custom-call(bf16[2,3,32,256]{3,2,1,0:T(8,128)(2,1)S(1)} %reshape.27.ck, f32[4,32,128]{2,1,0:T(8,128)S(1)} %bitcast.6, s32[4,32,128]{2,1,0:T(8,128)S(1)} %bitcast.7, f32[1,16]{1,0:T(1,128)S(1)} %bitcast.9), custom_call_target="tpu_custom_call" | custom-call | tf_op jit(solution)/shard_map/sweep/pallas_call | solution.py:497
  42.4 0.6 %copy.10 = f32[3,16,2,128]{3,2,1,0:T(2,128)} copy(f32[3,16,2,128]{3,2,1,0:T(2,128)S(1)} %bitcast.8) | data formatting | bytes 98304
  43.0 0.5 %copy.11 = f32[16]{0:T(128)} copy(f32[16]{0:T(128)S(1)} %bitcast.11) | data formatting | bytes 128
  43.6 0.5 %copy.12 = f32[16]{0:T(128)} copy(f32[16]{0:T(128)S(1)} %bitcast.10) | data formatting | bytes 128
Async XLA Ops:
  0.6 1.0 %copy-start = (f32[4,16,2,128]{3,2,1,0:T(2,128)S(1)}, f32[4,16,2,128]{3,2,1,0:T(2,128)}, u32[]{:S(2)}) copy-start(f32[4,16,2,128]{3,2,1,0:T(2,128)} %param.5) | copy-start | bytes 196612
  0.6 1.0 %copy-start.1 = (s32[4,16,2,128]{3,2,1,0:T(2,128)S(1)}, s32[4,16,2,128]{3,2,1,0:T(2,128)}, u32[]{:S(2)}) copy-start(s32[4,16,2,128]{3,2,1,0:T(2,128)} %param.6) | copy-start | bytes 196612
  0.7 1.0 %copy-start.2 = (f32[16]{0:T(128)S(1)}, f32[16]{0:T(128)}, u32[]{:S(2)}) copy-start(f32[16]{0:T(128)} %param.7) | copy-start | bytes 196

commit v2 on v1

--- a/solution.py
+++ b/solution.py
@@ -175,22 +175,29 @@
     theirs = pl.ds(pl.multiple_of(og * half, half), half)
     started = []
 
-    def put(src, dst, sem, where):
+    def put(src, dst, sem, where, when=None):
         copy = pltpu.make_async_remote_copy(
             src_ref=src, dst_ref=dst, send_sem=send.at[len(started)], recv_sem=sem,
             device_id=where, device_id_type=MESH,
         )
-        copy.start()
-        started.append(copy)
-
-    def arrived(dst, sem):
-        pltpu.make_async_remote_copy(
+        started.append((copy, when))
+        if when is None:
+            copy.start()
+        else:
+            pl.when(when)(copy.start)
+
+    def arrived(dst, sem, when=None):
+        copy = pltpu.make_async_remote_copy(
             src_ref=dst, dst_ref=dst, send_sem=send.at[0], recv_sem=sem,
             device_id={"gz": og}, device_id_type=MESH,
-        ).wait_recv()
+        )
+        if when is None:
+            copy.wait_recv()
+        else:
+            pl.when(when)(copy.wait_recv)
 
     z_peers = [lax.rem(x + d, zn) for d in range(1, zn)]
-    z_from = [lax.rem(x + zn - d, zn) for d in range(1, zn)]
+    has_next = {1: x + 1 < zn, -1: x > 0}
 
     barrier = pltpu.get_barrier_semaphore()
     for p in z_peers:
@@ -225,19 +232,23 @@
     own = [c * local_segs + j for j in range(local_segs)]
     far = [oc * local_segs + j for j in range(local_segs)]
 
-    for j in order:
-        for p in z_peers:
-            put(ck.at[j], ck_at(own[j], x, mine), rck.at[own[j], x, g], {"gx": p})
-        put(ck.at[j], ck_at(own[j], x, mine), rck.at[own[j], x, g], {"col": oc})
-    for b in range(2):
-        put(om_at(b, c, x, mine), om_at(b, c, x, mine), rom.at[b, c, x, g], {"col": oc})
-        for p in z_peers:
-            put(om_at(b, c, x, mine), om_at(b, c, x, mine), rom.at[b, c, x, g], {"gx": p})
-    put(dragb.at[mine], dragb.at[mine], rdrag, {"gz": og})
-    for j in order:
-        put(ck.at[j], ck_at(own[j], x, mine), rck.at[own[j], x, g], {"gz": og})
-    for b in range(2):
-        put(om_at(b, c, x, rim), om_at(b, c, x, rim), rom.at[b, c, x, g], {"gz": og})
+    def both_ways(src, dst, sem):
+        for way in (1, -1):
+            put(src, dst, sem, {"gx": x + way}, has_next[way])
+
+    waves = list(zip(order, range(2)))
+    for j, b in waves:
+        here, sem = ck_at(own[j], x, mine), rck.at[own[j], x, g]
+        both_ways(ck.at[j], here, sem)
+        put(ck.at[j], here, sem, {"col": oc})
+        part, sem_b = om_at(b, c, x, mine), rom.at[b, c, x, g]
+        put(part, part, sem_b, {"col": oc})
+        both_ways(part, part, sem_b)
+        put(ck.at[j], here, sem, {"gz": og})
+        edge = om_at(b, c, x, rim)
+        put(edge, edge, sem_b, {"gz": og})
+        if b == 0:
+            put(dragb.at[mine], dragb.at[mine], rdrag, {"gz": og})
     for j in order:
         ckg[own[j], :, x, mine, :] = ck[j]
 
@@ -245,34 +256,52 @@
     lam[...] = jnp.zeros_like(lam)
     acc[...] = jnp.zeros_like(acc)
 
-    for j in order:
-        for z in z_from:
+    def hop_ck(j, dist):
+        for way in (1, -1):
+            z = x - way * dist
+            there = (z >= 0) & (z < zn)
             here, sem = ck_at(own[j], z, mine), rck.at[own[j], z, g]
-            arrived(here, sem)
-            put(here, here, sem, {"col": oc})
-            put(here, here, sem, {"gz": og})
-    for b in range(2):
-        here, sem = om_at(b, oc, x, mine), rom.at[b, oc, x, g]
-        arrived(here, sem)
-        for p in z_peers:
-            put(here, here, sem, {"gx": p})
-        edge = om_at(b, oc, x, rim)
-        put(edge, edge, sem, {"gz": og})
-    for b in range(2):
-        for z in z_from:
-            arrived(om_at(b, c, z, mine), rom.at[b, c, z, g])
-            edge = om_at(b, c, z, rim)
-            put(edge, edge, rom.at[b, c, z, g], {"gz": og})
-    for j in order:
-        for z in range(zn):
-            here, sem = ck_at(far[j], z, mine), rck.at[far[j], z, g]
-            arrived(here, sem)
-            put(here, here, sem, {"gz": og})
-    for b in range(2):
-        for z in z_from:
-            arrived(om_at(b, oc, z, mine), rom.at[b, oc, z, g])
-            edge = om_at(b, oc, z, rim)
-            put(edge, edge, rom.at[b, oc, z, g], {"gz": og})
+            arrived(here, sem, there)
+            put(here, here, sem, {"gx": x + way}, there & has_next[way])
+            put(here, here, sem, {"col": oc}, there)
+            put(here, here, sem, {"gz": og}, there)
+
+    def hop_om(b, col, dist):
+        for way in (1, -1):
+            z = x - way * dist
+            there = (z >= 0) & (z < zn)
+            here, sem = om_at(b, col, z, mine), rom.at[b, col, z, g]
+            arrived(here, sem, there)
+            put(here, here, sem, {"gx": x + way}, there & has_next[way])
+            edge = om_at(b, col, z, rim)
+            put(edge, edge, sem, {"gz": og}, there)
+
+    def pieces(j, b):
+        for dist in range(1, zn + 1):
+            def part(dist=dist):
+                if dist < zn:
+                    hop_ck(j, dist)
+                    hop_om(b, c, dist)
+                if dist == 1:
+                    here, sem = om_at(b, oc, x, mine), rom.at[b, oc, x, g]
+                    arrived(here, sem)
+                    both_ways(here, here, sem)
+                    edge = om_at(b, oc, x, rim)
+                    put(edge, edge, sem, {"gz": og})
+                else:
+                    hop_om(b, oc, dist - 1)
+            yield part
+
+        def rest():
+            for z in range(zn):
+                here, sem = ck_at(far[j], z, mine), rck.at[far[j], z, g]
+                arrived(here, sem)
+                put(here, here, sem, {"gz": og})
+        yield rest
+
+    for part in pieces(*waves[0]):
+        part()
+    pending = [part for wave in waves[1:] for part in pieces(*wave)]
     arrived(dragb.at[theirs], rdrag)
 
     at_lane = lax.broadcasted_iota(jnp.int32, (TILE, wide), 1)
@@ -419,11 +448,15 @@
             return carry
 
         lax.fori_loop(0, count, body, 0)
+        if pending:
+            pending.pop(0)()
 
     now = 0
     for seg in reversed(range(segments)):
         remaining = SEG * (seg + 1)
         owner, b = seg // local_segs, 0 if seg >= segments // 2 else 1
+        while pending and seg < segments - 1:
+            pending.pop(0)()
         for z in range(zn):
             arrived(ck_at(seg, z, theirs), rck.at[seg, z, og])
         if seg == segments - 1 or seg == segments // 2 - 1:
@@ -484,15 +517,18 @@
         sums = jnp.sum(acc[k, mine, :], axis=1, keepdims=True)
         line = jnp.sum(jnp.where(pick, sums, 0.0), axis=0, keepdims=True)
         ref[...] = factor * line[:, :levels]
-    for copy in started:
-        copy.wait_send()
+    for copy, when in started:
+        if when is None:
+            copy.wait_send()
+        else:
+            pl.when(when)(copy.wait_send)
 
 
 def gathered(zn, checkpoints, obs_values, obs_mask, drag):
     segments, levels, lat, lon = obs_values.shape
     half, wide = levels * lat, 2 * lon
     local_segs = checkpoints.shape[0]
-    sends = local_segs * ((zn + 1) + 2 * (zn - 1) + zn) + 2 * (zn + 1 + zn + 2 * (zn - 1)) + 1
+    sends = local_segs * (12 + 20 * zn)
     f32 = jnp.float32
     out, cost, pull = pl.pallas_call(
         functools.partial(sweep_kernel, zn, levels, lat, lon),
@@ -510,7 +546,7 @@
             pltpu.VMEM((2, 3, zn + 2, 2, 2 * half + 2 * PAD, lon), f32),
             pltpu.VMEM((2, 3, zn + 2, 2, 2 * half + 2 * PAD, lon), f32),
             pltpu.VMEM((2, 2 * half, wide), f32),
-            pltpu.SemaphoreType.DMA((sends + 8,)),
+            pltpu.SemaphoreType.DMA((sends,)),
             pltpu.SemaphoreType.DMA((segments, zn, 2)),
             pltpu.SemaphoreType.DMA((2, 2, zn, 2)),
             pltpu.SemaphoreType.DMA,
@@ -542,7 +578,7 @@
         and lat <= PAD
         and half % (4 * TILE) == 0
         and lon == 128
-        and segments % 2 == 0
+        and segments == 2 * checkpoints.shape[0] == 4
         and levels >= 2 * (SEG * segments + 1) - levels
         and half // 2 >= SEG * segments * lat
         and levels <= lon

time: 44.3 us -> 46 us (1.038)
  Pallas kernels: 40.7 us -> 42.5 us
    pallas_call x1, Pallas kernels: 40.7 us -> 42.5 us  [gathered(): pl.pallas_call(functools.partial(sweep_kernel, zn, levels, lat, lon), out...]
where the time goes in v2:
time: 46 us; the launch traced here: 45.8 us
  Pallas kernels  42.5 us (92%)
  local copies, waits for them, and re-layouts  2.64 us (6%)
  between operations  0.69 us (2%)
    pallas_call x1, Pallas kernels, gathered(): pl.pallas_call(functools.partial(sweep_kernel, zn, levels, lat, lon), out...  42.5 us
    unnamed x9, local copies, waits for them, and re-layouts  1.66 us
    reshape x1, local copies, waits for them, and re-layouts, gathered(): checkpoints.reshape(local_segs, 3, half, wide)  0.98 us

profile of v2, /device:TPU:1, one launch (start us, length us, event | category | flops | bytes accessed | tf_op | source)
XLA Modules:
  0.0 45.8 jit_solution(1928639175337561653)
XLA Ops:
  0.6 0.0 copy-start
  0.6 0.0 copy-start.1
  0.7 0.0 copy-start.2
  0.7 1.0 %reshape.27.ck = bf16[2,3,32,256]{3,2,1,0:T(8,128)(2,1)S(1)} reshape(bf16[2,3,16,2,256]{4,3,2,1,0:T(2,128)(2,1)} %param.4) | data formatting | bytes 196608 | tf_op jit(solution)/shard_map/reshape | solution.py:559
  1.6 0.0 copy-done
  1.7 0.0 copy-done.1
  1.7 0.0 copy-done.2
  1.7 42.5 %sweep.1 = (f32[3,32,128]{2,1,0:T(8,128)S(1)}, f32[1,16]{1,0:T(1,128)S(1)}, f32[1,16]{1,0:T(1,128)S(1)}) custom-call(bf16[2,3,32,256]{3,2,1,0:T(8,128)(2,1)S(1)} %reshape.27.ck, f32[4,32,128]{2,1,0:T(8,128)S(1)} %bitcast.6, s32[4,32,128]{2,1,0:T(8,128)S(1)} %bitcast.7, f32[1,16]{1,0:T(1,128)S(1)} %bitcast.9), custom_call_target="tpu_custom_call" | custom-call | tf_op jit(solution)/shard_map/sweep/pallas_call | solution.py:533
  44.2 0.6 %copy.10 = f32[3,16,2,128]{3,2,1,0:T(2,128)} copy(f32[3,16,2,128]{3,2,1,0:T(2,128)S(1)} %bitcast.8) | data formatting | bytes 98304
  44.8 0.5 %copy.11 = f32[16]{0:T(128)} copy(f32[16]{0:T(128)S(1)} %bitcast.11) | data formatting | bytes 128
  45.3 0.5 %copy.12 = f32[16]{0:T(128)} copy(f32[16]{0:T(128)S(1)} %bitcast.10) | data formatting | bytes 128
Async XLA Ops:
  0.6 1.0 %copy-start = (f32[4,16,2,128]{3,2,1,0:T(2,128)S(1)}, f32[4,16,2,128]{3,2,1,0:T(2,128)}, u32[]{:S(2)}) copy-start(f32[4,16,2,128]{3,2,1,0:T(2,128)} %param.5) | copy-start | bytes 196612
  0.6 1.0 %copy-start.1 = (s32[4,16,2,128]{3,2,1,0:T(2,128)S(1)}, s32[4,16,2,128]{3,2,1,0:T(2,128)}, u32[]{:S(2)}) copy-start(s32[4,16,2,128]{3,2,1,0:T(2,128)} %param.6) | copy-start | bytes 196612
  0.7 1.0 %copy-start.2 = (f32[16]{0:T(128)S(1)}, f32[16]{0:T(128)}, u32[]{:S(2)}) copy-start(f32[16]{0:T(128)} %param.7) | copy-start | bytes 196

commit v3 on v2

--- a/solution.py
+++ b/solution.py
@@ -197,7 +197,7 @@
             pl.when(when)(copy.wait_recv)
 
     z_peers = [lax.rem(x + d, zn) for d in range(1, zn)]
-    has_next = {1: x + 1 < zn, -1: x > 0}
+    z_from = [lax.rem(x + zn - d, zn) for d in range(1, zn)]
 
     barrier = pltpu.get_barrier_semaphore()
     for p in z_peers:
@@ -232,23 +232,29 @@
     own = [c * local_segs + j for j in range(local_segs)]
     far = [oc * local_segs + j for j in range(local_segs)]
 
-    def both_ways(src, dst, sem):
-        for way in (1, -1):
-            put(src, dst, sem, {"gx": x + way}, has_next[way])
-
-    waves = list(zip(order, range(2)))
-    for j, b in waves:
-        here, sem = ck_at(own[j], x, mine), rck.at[own[j], x, g]
-        both_ways(ck.at[j], here, sem)
-        put(ck.at[j], here, sem, {"col": oc})
-        part, sem_b = om_at(b, c, x, mine), rom.at[b, c, x, g]
-        put(part, part, sem_b, {"col": oc})
-        both_ways(part, part, sem_b)
-        put(ck.at[j], here, sem, {"gz": og})
+    def to_rows(src, dst, sem):
+        for p in z_peers:
+            put(src, dst, sem, {"gx": p})
+
+    def own_ck(j):
+        return ck.at[j], ck_at(own[j], x, mine), rck.at[own[j], x, g]
+
+    def own_om(b):
+        part = om_at(b, c, x, mine)
+        return part, part, rom.at[b, c, x, g]
+
+    def own_edge(b):
         edge = om_at(b, c, x, rim)
-        put(edge, edge, sem_b, {"gz": og})
-        if b == 0:
-            put(dragb.at[mine], dragb.at[mine], rdrag, {"gz": og})
+        put(edge, edge, rom.at[b, c, x, g], {"gz": og})
+
+    newest = order[0]
+    put(*own_om(0), {"col": oc})
+    to_rows(*own_ck(newest))
+    put(*own_ck(newest), {"col": oc})
+    to_rows(*own_om(0))
+    put(*own_ck(newest), {"gz": og})
+    put(dragb.at[mine], dragb.at[mine], rdrag, {"gz": og})
+    own_edge(0)
     for j in order:
         ckg[own[j], :, x, mine, :] = ck[j]
 
@@ -256,53 +262,58 @@
     lam[...] = jnp.zeros_like(lam)
     acc[...] = jnp.zeros_like(acc)
 
-    def hop_ck(j, dist):
-        for way in (1, -1):
-            z = x - way * dist
-            there = (z >= 0) & (z < zn)
-            here, sem = ck_at(own[j], z, mine), rck.at[own[j], z, g]
-            arrived(here, sem, there)
-            put(here, here, sem, {"gx": x + way}, there & has_next[way])
-            put(here, here, sem, {"col": oc}, there)
-            put(here, here, sem, {"gz": og}, there)
-
-    def hop_om(b, col, dist):
-        for way in (1, -1):
-            z = x - way * dist
-            there = (z >= 0) & (z < zn)
-            here, sem = om_at(b, col, z, mine), rom.at[b, col, z, g]
-            arrived(here, sem, there)
-            put(here, here, sem, {"gx": x + way}, there & has_next[way])
+    def pass_ck(j, z):
+        here, sem = ck_at(own[j], z, mine), rck.at[own[j], z, g]
+        arrived(here, sem)
+        put(here, here, sem, {"col": oc})
+        put(here, here, sem, {"gz": og})
+
+    def pass_far(j):
+        for z in [x] + z_from:
+            here, sem = ck_at(far[j], z, mine), rck.at[far[j], z, g]
+            arrived(here, sem)
+            put(here, here, sem, {"gz": og})
+
+    def pass_side(b):
+        here, sem = om_at(b, oc, x, mine), rom.at[b, oc, x, g]
+        arrived(here, sem)
+        to_rows(here, here, sem)
+        edge = om_at(b, oc, x, rim)
+        put(edge, edge, sem, {"gz": og})
+
+    def pass_om(b, col):
+        for z in z_from:
+            arrived(om_at(b, col, z, mine), rom.at[b, col, z, g])
             edge = om_at(b, col, z, rim)
-            put(edge, edge, sem, {"gz": og}, there)
-
-    def pieces(j, b):
-        for dist in range(1, zn + 1):
-            def part(dist=dist):
-                if dist < zn:
-                    hop_ck(j, dist)
-                    hop_om(b, c, dist)
-                if dist == 1:
-                    here, sem = om_at(b, oc, x, mine), rom.at[b, oc, x, g]
-                    arrived(here, sem)
-                    both_ways(here, here, sem)
-                    edge = om_at(b, oc, x, rim)
-                    put(edge, edge, sem, {"gz": og})
-                else:
-                    hop_om(b, oc, dist - 1)
-            yield part
-
-        def rest():
-            for z in range(zn):
-                here, sem = ck_at(far[j], z, mine), rck.at[far[j], z, g]
-                arrived(here, sem)
-                put(here, here, sem, {"gz": og})
-        yield rest
-
-    for part in pieces(*waves[0]):
-        part()
-    pending = [part for wave in waves[1:] for part in pieces(*wave)]
+            put(edge, edge, rom.at[b, col, z, g], {"gz": og})
+
+    def start_late():
+        for j in order[1:]:
+            to_rows(*own_ck(j))
+            put(*own_ck(j), {"col": oc})
+            put(*own_ck(j), {"gz": og})
+        put(*own_om(1), {"col": oc})
+        to_rows(*own_om(1))
+        own_edge(1)
+
+    pass_side(0)
+    for z in z_from:
+        pass_ck(newest, z)
+    start_late()
+    pass_om(0, c)
+    pass_far(newest)
+    pass_om(0, oc)
     arrived(dragb.at[theirs], rdrag)
+    pending = []
+    for j in order[1:]:
+        pending.append(lambda j=j: [pass_ck(j, z) for z in z_from])
+    pending.append(lambda: pass_side(1))
+    for j in order[1:]:
+        pending.append(lambda j=j: pass_far(j))
+    before_second = len(pending)
+    pending.append(lambda: pass_om(1, c))
+    pending.append(lambda: pass_om(1, oc))
+    waiting_parts = len(pending)
 
     at_lane = lax.broadcasted_iota(jnp.int32, (TILE, wide), 1)
     at_row = lax.broadcasted_iota(jnp.int32, (TILE, wide), 0) % lat
@@ -455,7 +466,10 @@
     for seg in reversed(range(segments)):
         remaining = SEG * (seg + 1)
         owner, b = seg // local_segs, 0 if seg >= segments // 2 else 1
-        while pending and seg < segments - 1:
+        due = 0 if seg == segments - 1 else before_second
+        if seg < segments // 2:
+            due = waiting_parts
+        while waiting_parts - len(pending) < due:
             pending.pop(0)()
         for z in range(zn):
             arrived(ck_at(seg, z, theirs), rck.at[seg, z, og])

time: 46 us -> 42.7 us (0.928)
  Pallas kernels: 42.5 us -> 38.9 us
    pallas_call x1, Pallas kernels: 42.5 us -> 38.9 us  [gathered(): pl.pallas_call(functools.partial(sweep_kernel, zn, levels, lat, lon), out...]
where the time goes in v3:
time: 42.7 us; the launch traced here: 42.3 us
  Pallas kernels  38.9 us (91%)
  local copies, waits for them, and re-layouts  2.64 us (6%)
  between operations  0.69 us (2%)
    pallas_call x1, Pallas kernels, gathered(): pl.pallas_call(functools.partial(sweep_kernel, zn, levels, lat, lon), out...  38.9 us
    unnamed x9, local copies, waits for them, and re-layouts  1.66 us
    reshape x1, local copies, waits for them, and re-layouts, gathered(): checkpoints.reshape(local_segs, 3, half, wide)  0.98 us

profile of v3, /device:TPU:1, one launch (start us, length us, event | category | flops | bytes accessed | tf_op | source)
XLA Modules:
  0.0 42.3 jit_solution(8239915535271729377)
XLA Ops:
  0.6 0.0 copy-start
  0.6 0.0 copy-start.1
  0.7 0.0 copy-start.2
  0.7 1.0 %reshape.27.ck = bf16[2,3,32,256]{3,2,1,0:T(8,128)(2,1)S(1)} reshape(bf16[2,3,16,2,256]{4,3,2,1,0:T(2,128)(2,1)} %param.4) | data formatting | bytes 196608 | tf_op jit(solution)/shard_map/reshape | solution.py:573
  1.6 0.0 copy-done
  1.7 0.0 copy-done.1
  1.7 0.0 copy-done.2
  1.7 38.9 %sweep.1 = (f32[3,32,128]{2,1,0:T(8,128)S(1)}, f32[1,16]{1,0:T(1,128)S(1)}, f32[1,16]{1,0:T(1,128)S(1)}) custom-call(bf16[2,3,32,256]{3,2,1,0:T(8,128)(2,1)S(1)} %reshape.27.ck, f32[4,32,128]{2,1,0:T(8,128)S(1)} %bitcast.6, s32[4,32,128]{2,1,0:T(8,128)S(1)} %bitcast.7, f32[1,16]{1,0:T(1,128)S(1)} %bitcast.9), custom_call_target="tpu_custom_call" | custom-call | tf_op jit(solution)/shard_map/sweep/pallas_call | solution.py:547
  40.6 0.6 %copy.10 = f32[3,16,2,128]{3,2,1,0:T(2,128)} copy(f32[3,16,2,128]{3,2,1,0:T(2,128)S(1)} %bitcast.8) | data formatting | bytes 98304
  41.2 0.5 %copy.11 = f32[16]{0:T(128)} copy(f32[16]{0:T(128)S(1)} %bitcast.11) | data formatting | bytes 128
  41.7 0.5 %copy.12 = f32[16]{0:T(128)} copy(f32[16]{0:T(128)S(1)} %bitcast.10) | data formatting | bytes 128
Async XLA Ops:
  0.6 1.0 %copy-start = (f32[4,16,2,128]{3,2,1,0:T(2,128)S(1)}, f32[4,16,2,128]{3,2,1,0:T(2,128)}, u32[]{:S(2)}) copy-start(f32[4,16,2,128]{3,2,1,0:T(2,128)} %param.5) | copy-start | bytes 196612
  0.6 1.0 %copy-start.1 = (s32[4,16,2,128]{3,2,1,0:T(2,128)S(1)}, s32[4,16,2,128]{3,2,1,0:T(2,128)}, u32[]{:S(2)}) copy-start(s32[4,16,2,128]{3,2,1,0:T(2,128)} %param.6) | copy-start | bytes 196612
  0.7 1.0 %copy-start.2 = (f32[16]{0:T(128)S(1)}, f32[16]{0:T(128)}, u32[]{:S(2)}) copy-start(f32[16]{0:T(128)} %param.7) | copy-start | bytes 196

commit v4 on v3

--- a/solution.py
+++ b/solution.py
@@ -323,6 +323,8 @@
     total_lat, total_lon = float(zn * lat), float(wide)
     col_weight = 1.0 + 2.0 * at_lane.astype(jnp.float32) / total_lon
     coriolis = [time_step * (0.2 + 0.1 * (row_f + float(z * lat)) / total_lat) for z in range(zn)]
+    own_row = (at_row + x * lat).astype(jnp.float32)
+    own_turn = time_step * (0.2 + 0.1 * own_row / total_lat)
     weights = [(1.0 + 2.0 * (row_f + float(z * lat)) / total_lat) * col_weight for z in range(zn)]
     half_step = 0.5 * time_step
     keep = 1.0 - 4.0 * viscosity - 2.0 * vertical_mix
@@ -403,7 +405,7 @@
             + vertical_mix * mixed(xs, src, 0, z, o)
         )
 
-    def adjoint(src, lead, z, o, dt_drag):
+    def adjoint(src, lead, z, o, dt_drag, turn):
         h, u, v = (at(xs, src, f, z, o, 0) for f in range(3))
         a, b, d = (at(lam, lead, f, z, o, 0) for f in range(3))
         u_e, v_e, u_w, v_w = east(u), east(v), west(u), west(v)
@@ -431,7 +433,7 @@
                 + deep * a_dx
                 - (b * (u_e - u_w) + d * (v_e - v_w))
             )
-            - (dt_drag * b + coriolis[z] * d)
+            - (dt_drag * b + turn * d)
             + vertical_mix * mixed(lam, lead, 1, z, o)
         )
         new_d = (
@@ -444,7 +446,7 @@
                 + deep * a_dy
                 - (b * (u_n - u_s) + d * (v_n - v_s))
             )
-            + (coriolis[z] * b - dt_drag * d)
+            + (turn * b - dt_drag * d)
             + vertical_mix * mixed(lam, lead, 2, z, o)
         )
         return (new_a, new_b, new_d), u * b + v * d
@@ -511,11 +513,19 @@
             def back(m):
                 dt_drag = rates(m)
                 pull = jnp.zeros((TILE, wide), jnp.float32)
-                for z in range(zn):
-                    new, part = adjoint(n, now, z, m + PAD, dt_drag)
+                for z in range(zn) if remaining else ():
+                    new, part = adjoint(n, now, z, m + PAD, dt_drag, coriolis[z])
                     pull = pull + part
                     for f, value in enumerate(new):
                         keep_at(lam, later, f, z, m, value)
+                if not remaining:
+                    spot = pl.multiple_of(m + PAD, TILE)
+                    for z in range(zn):
+                        for f in (1, 2):
+                            pull = pull + at(xs, n, f, z, spot, 0) * at(lam, now, f, z, spot, 0)
+                    new, unused = adjoint(n, now, x, m + PAD, dt_drag, own_turn)
+                    for f, value in enumerate(new):
+                        keep_at(lam, later, f, x, m, value)
                 acc[1, pl.ds(m, TILE), :] = acc[1, pl.ds(m, TILE), :] + pull
 
             over(remaining, back)

time: 42.7 us -> 42.4 us (level)
  no operation moved by 1% of the time
where the time goes in v4:
time: 42.4 us; the launch traced here: 41.9 us
  Pallas kernels  38.6 us (91%)
  local copies, waits for them, and re-layouts  2.64 us (6%)
  between operations  0.69 us (2%)
    pallas_call x1, Pallas kernels, gathered(): pl.pallas_call(functools.partial(sweep_kernel, zn, levels, lat, lon), out...  38.6 us
    unnamed x9, local copies, waits for them, and re-layouts  1.66 us
    reshape x1, local copies, waits for them, and re-layouts, gathered(): checkpoints.reshape(local_segs, 3, half, wide)  0.98 us

profile of v4, /device:TPU:1, one launch (start us, length us, event | category | flops | bytes accessed | tf_op | source)
XLA Modules:
  0.0 41.9 jit_solution(11989949967536404001)
XLA Ops:
  0.6 0.0 copy-start
  0.6 0.0 copy-start.1
  0.7 0.0 copy-start.2
  0.7 1.0 %reshape.27.ck = bf16[2,3,32,256]{3,2,1,0:T(8,128)(2,1)S(1)} reshape(bf16[2,3,16,2,256]{4,3,2,1,0:T(2,128)(2,1)} %param.4) | data formatting | bytes 196608 | tf_op jit(solution)/shard_map/reshape | solution.py:583
  1.6 0.0 copy-done
  1.7 0.0 copy-done.1
  1.7 0.0 copy-done.2
  1.7 38.6 %sweep.1 = (f32[3,32,128]{2,1,0:T(8,128)S(1)}, f32[1,16]{1,0:T(1,128)S(1)}, f32[1,16]{1,0:T(1,128)S(1)}) custom-call(bf16[2,3,32,256]{3,2,1,0:T(8,128)(2,1)S(1)} %reshape.27.ck, f32[4,32,128]{2,1,0:T(8,128)S(1)} %bitcast.6, s32[4,32,128]{2,1,0:T(8,128)S(1)} %bitcast.7, f32[1,16]{1,0:T(1,128)S(1)} %bitcast.9), custom_call_target="tpu_custom_call" | custom-call | tf_op jit(solution)/shard_map/sweep/pallas_call | solution.py:557
  40.3 0.6 %copy.10 = f32[3,16,2,128]{3,2,1,0:T(2,128)} copy(f32[3,16,2,128]{3,2,1,0:T(2,128)S(1)} %bitcast.8) | data formatting | bytes 98304
  40.9 0.5 %copy.11 = f32[16]{0:T(128)} copy(f32[16]{0:T(128)S(1)} %bitcast.11) | data formatting | bytes 128
  41.4 0.5 %copy.12 = f32[16]{0:T(128)} copy(f32[16]{0:T(128)S(1)} %bitcast.10) | data formatting | bytes 128
Async XLA Ops:
  0.6 1.0 %copy-start = (f32[4,16,2,128]{3,2,1,0:T(2,128)S(1)}, f32[4,16,2,128]{3,2,1,0:T(2,128)}, u32[]{:S(2)}) copy-start(f32[4,16,2,128]{3,2,1,0:T(2,128)} %param.5) | copy-start | bytes 196612
  0.6 1.0 %copy-start.1 = (s32[4,16,2,128]{3,2,1,0:T(2,128)S(1)}, s32[4,16,2,128]{3,2,1,0:T(2,128)}, u32[]{:S(2)}) copy-start(s32[4,16,2,128]{3,2,1,0:T(2,128)} %param.6) | copy-start | bytes 196612
  0.7 1.0 %copy-start.2 = (f32[16]{0:T(128)S(1)}, f32[16]{0:T(128)}, u32[]{:S(2)}) copy-start(f32[16]{0:T(128)} %param.7) | copy-start | bytes 196
